TPU v7x, 32 devices: a whole 2x2x4 slice. The times are simulated.
32 devices in a mesh: elem: 16 (over z, y, x), param: 2 (over core).
Axes of the slice: x: 2, y: 2, z: 4, core: 2. Of those that a mesh axis runs over, the one named last changes fastest.
Arguments:
- coords: bfloat16 [8, 300], P('param'), may hold values from -6 to 6
- basis_rows: bfloat16 [3, 300, 4096], P(None, None, 'elem'), may hold values from -0.375 to 0.375
- connectivity: int32 [4096, 8], P(('elem', 'param')), may hold values from 0 to 319, as said below
- modulus: float32 [4096], P(('elem', 'param')), may hold values from 0.5 to 15
- stiffness: float32 [24, 24], replicated, may hold values from -1.25 to 1.25
Outputs:
- training: bfloat16 [8, 300, 4096], P(None, None, ('elem', 'param'))
- target: float32 [8, 300], replicated
Inputs may be any that keep to these rules, and one draw needn't show every extreme that they name: `connectivity`: A number c of 256 or more names node c - 256 of the next node block; the last block's next block is the first. An element's eight corner numbers lie among min(8, 64) consecutive numbers; where these lie in the block is not tied to the element's position.
All inputs are finite; a program needn't handle non-finite values.
Results may differ from a plain program's by a relative error of at most 0.0072.
Values may be sent and summed in bfloat16 or wider, within the bound.
A program may use at most 64 MiB of HBM per device.

v0:
```python
import functools
import math

import jax
import jax.numpy as jnp
from jax import lax
from jax.experimental import pallas as pl
from jax.experimental.pallas import tpu as pltpu
from jax.sharding import PartitionSpec as P

MESH = pl.DeviceIdType.MESH
F32 = jnp.float32
BF16 = jnp.bfloat16


def round_up(value, to):
    return -(-value // to) * to


def kernel(
    elems, params, inner,
    own_snaps, modes, dofs,
    small_ref, basis_hbm,
    cols_ref, flat_ref,
    basis_ref,
    packed, ghost_in, ghost, disp, mask, weights, ghost_weights, acc, part, part_p, part_i, part_o,
    load, send_g, recv_g, send_d, recv_d, send_n, recv_n, send_p, recv_p, send_i, recv_i, send_o, recv_o,
):
    outer = elems // inner
    snaps = own_snaps * params
    nodes = basis_hbm.shape[2]
    ghosts = nodes // 4
    total_nodes = nodes + ghosts
    count = cols_ref.shape[1]
    me_e, me_p = lax.axis_index("elem"), lax.axis_index("param")
    me_i, me_o = me_e % inner, me_e // inner
    before, after = (me_e + elems - 1) % elems, (me_e + 1) % elems

    def peers(me, size):
        return [((me + j) % size, (me + size - j) % size) for j in range(1, size)]

    def inner_id(i):
        return (me_o * inner + i, me_p)

    def outer_id(o):
        return (o * inner + me_i, me_p)

    barrier = pltpu.get_barrier_semaphore()
    near = [(before, p) for p in range(params)] + [(after, p) for p in range(params)]
    near += [(me_e, to) for to, _ in peers(me_p, params)]
    near += [inner_id(to) for to, _ in peers(me_i, inner)]
    near += [outer_id(to) for to, _ in peers(me_o, outer)]
    for device in near:
        pl.semaphore_signal(barrier, inc=1, device_id=device, device_id_type=MESH)

    loads = [
        pltpu.make_async_copy(
            basis_hbm.at[k], basis_ref.at[:, pl.ds(k * nodes, nodes)], load.at[k]
        )
        for k in range(3)
    ]
    for copy in loads:
        copy.start()

    def remote(src, dst, send, recv, device):
        return pltpu.make_async_remote_copy(
            src_ref=src, dst_ref=dst, send_sem=send, recv_sem=recv,
            device_id=device, device_id_type=MESH,
        )

    own_tiles = nodes // 128
    ghost_tiles = disp.shape[1] - own_tiles
    half = packed.shape[1]
    split = half < modes
    conn_at, mod_at, coords_at = dofs, dofs + 8, dofs + 16
    coords = small_ref[coords_at : coords_at + own_snaps, :modes].astype(BF16)
    for k in range(3):
        loads[k].wait()
        moved = jnp.dot(
            coords, basis_ref[:, k * nodes : (k + 1) * nodes], preferred_element_type=F32
        )
        moved = moved.astype(BF16).astype(F32)
        for t in range(own_tiles):
            disp[me_p, t, k] = moved[:, t * 128 : (t + 1) * 128]
    for k in range(3):
        at = k * nodes
        if split:
            packed[k, :, :ghosts] = basis_ref[:half, at : at + ghosts]
            packed[k, : modes - half, ghosts:] = basis_ref[half:, at : at + ghosts]
        else:
            packed[k, :modes] = basis_ref[:, at : at + ghosts]

    pl.semaphore_wait(barrier, len(near))
    own_part, ghost_part = pl.ds(0, own_tiles), pl.ds(own_tiles, ghost_tiles)
    sends, arrivals = [], []
    for p in range(params):
        turn = (me_p + p) % params
        source = (me_p + params - p) % params
        sends.append(remote(
            disp.at[me_p, pl.ds(0, ghost_tiles)], disp.at[me_p, ghost_part],
            send_d.at[p], recv_d.at[me_p], (before, turn),
        ))
        arrivals.append(remote(
            disp.at[source, pl.ds(0, ghost_tiles)], disp.at[source, ghost_part],
            send_d.at[p], recv_d.at[source], (before, turn),
        ))
        if p:
            sends.append(remote(
                disp.at[me_p, own_part], disp.at[me_p, own_part],
                send_n.at[p], recv_n.at[me_p], (me_e, turn),
            ))
            arrivals.append(remote(
                disp.at[source, own_part], disp.at[source, own_part],
                send_n.at[p], recv_n.at[source], (me_e, turn),
            ))
    ghost_copy = remote(packed, ghost_in, send_g, recv_g, (before, me_p))
    for copy in sends + [ghost_copy]:
        copy.start()

    corners = small_ref[conn_at : conn_at + 8, :count].astype(jnp.int32)
    base = jnp.min(corners, axis=0, keepdims=True)
    residue = corners % 8
    lane_at = corners % 128
    tile_at = corners // 128
    node = lax.broadcasted_iota(jnp.int32, (total_nodes, count), 0)
    inside = (node >= base) & (node < base + 8)
    mask[...] = jnp.where(inside, 1.0, 0.0).astype(BF16)
    stiff = small_ref[:dofs, :dofs]
    high = stiff.astype(BF16)
    rest = stiff - high.astype(F32)
    mid = rest.astype(BF16)
    low = (rest - mid.astype(F32)).astype(BF16)
    modulus = small_ref[mod_at : mod_at + 1, :count]
    modulus2 = jnp.concatenate([modulus, modulus], axis=1)
    part[...] = jnp.zeros_like(part)
    lane = lax.broadcasted_iota(jnp.int32, (1, 128), 1)
    row8 = lax.broadcasted_iota(jnp.int32, (8, count), 0)

    for copy in arrivals:
        copy.wait_recv()

    def own_product(p):
        pieces = []
        for at in range(2):
            s = 2 * p + at
            rows = []
            for k in range(3):
                found = jnp.zeros((8, count), F32)
                for t in range(disp.shape[1]):
                    line = disp[s // own_snaps, t, k, pl.ds(s % own_snaps, 1), :]
                    got = jnp.take_along_axis(jnp.broadcast_to(line, (8, 128)), lane_at, axis=1)
                    found = jnp.where(tile_at == t, got, found)
                rows.append(found)
            pieces.append(jnp.concatenate(rows, axis=0))
        moved = jnp.concatenate(pieces, axis=1)
        moved16 = moved.astype(BF16)
        linear = jnp.dot(low, moved16, preferred_element_type=F32)
        linear = linear + jnp.dot(mid, moved16, preferred_element_type=F32)
        linear = linear + jnp.dot(high, moved16, preferred_element_type=F32)
        forces = (modulus2 * (linear + 0.25 * moved * moved * moved)).astype(BF16).astype(F32)
        for at in range(2):
            for k in range(3):
                spread = jnp.zeros((8, count), F32)
                for a in range(8):
                    force = forces[k * 8 + a : k * 8 + a + 1, at * count : (at + 1) * count]
                    spread = spread + jnp.where(residue[a : a + 1] == row8, force, 0.0)
                twice = jnp.concatenate([spread, spread], axis=0).astype(BF16)
                tall = jnp.concatenate([twice] * (total_nodes // 16), axis=0) * mask[...]
                columns = slice(at * count, (at + 1) * count)
                weights[k * nodes : (k + 1) * nodes, columns] = tall[:nodes]
                ghost_weights[p, k * ghosts : (k + 1) * ghosts, columns] = tall[nodes:]
        acc[p] = jnp.dot(basis_ref[...], weights[...], preferred_element_type=F32)

    def whole_product(p, sums):
        result = acc[p] + jnp.dot(ghost[...], ghost_weights[p], preferred_element_type=F32)
        for at in range(2):
            s = 2 * p + at
            mine = result[:, at * count : (at + 1) * count]
            cols_ref[pl.ds(s, modes, stride=snaps), :] = mine
            norm = jnp.sqrt(jnp.sum(mine * mine, axis=0, keepdims=True))
            norm = jnp.sum(norm, axis=1, keepdims=True)
            line = jnp.concatenate([jnp.sum(mine, axis=1, keepdims=True), norm], axis=0)
            sums = jnp.where(lane == s, line, sums)
        return sums

    pairs = snaps // 2
    if pairs <= 4:
        for p in range(pairs):
            own_product(p)
    else:
        lax.fori_loop(0, pairs, lambda p, c: (own_product(p), c)[1], 0)

    ghost_copy.wait_recv()
    for k in range(3):
        if split:
            ghost[:half, k * ghosts : (k + 1) * ghosts] = ghost_in[k, :, :ghosts]
            ghost[half:, k * ghosts : (k + 1) * ghosts] = ghost_in[k, : modes - half, ghosts:]
        else:
            ghost[:, k * ghosts : (k + 1) * ghosts] = ghost_in[k, :modes]
    sums = jnp.zeros((modes + 1, 128), F32)
    if pairs <= 4:
        for p in range(pairs):
            sums = whole_product(p, sums)
    else:
        sums = lax.fori_loop(0, pairs, whole_product, sums)

    wide = part_p.shape[2]
    part[: modes + 1] = sums
    flat = jnp.concatenate(
        [jnp.transpose(part[t * 128 : (t + 1) * 128])[:snaps] for t in range(wide // 128)], axis=1
    )
    waits = sends + [ghost_copy]

    def reduced(value, ref, me, size, device_of, send, recv):
        ref[me] = value
        arriving = []
        for j, (to, source) in enumerate(peers(me, size)):
            out = remote(ref.at[me], ref.at[me], send.at[j], recv.at[me], device_of(to))
            out.start()
            waits.append(out)
            arriving.append(remote(
                ref.at[source], ref.at[source], send.at[j], recv.at[source], device_of(to)
            ))
        for copy in arriving:
            copy.wait_recv()
        total = ref[0]
        for j in range(1, size):
            total = total + ref[j]
        return total

    flat = reduced(flat, part_p, me_p, params, lambda p: (me_e, p), send_p, recv_p)
    flat = reduced(flat, part_i, me_i, inner, inner_id, send_i, recv_i)
    flat = reduced(flat, part_o, me_o, outer, outer_id, send_o, recv_o)
    flat_ref[...] = flat
    for copy in waits:
        copy.wait_send()


def finish_kernel(elem_total, cols_ref, flat_ref, training_hbm, target_hbm, training, target, sem):
    snaps, modes = target.shape
    row_scale = flat_ref[:, modes : modes + 1] / elem_total
    target[...] = flat_ref[:, :modes] / (row_scale * math.sqrt(elem_total))
    copies = [pltpu.make_async_copy(target, target_hbm, sem.at[0])]
    copies[0].start()
    inverse = jnp.broadcast_to(1.0 / row_scale, (snaps, training.shape[2]))
    chunks = sem.shape[0] - 1
    size = modes // chunks
    for c in range(chunks):
        piece = cols_ref[c * size * snaps : (c + 1) * size * snaps]
        piece = piece.reshape(size, snaps, training.shape[2]) * inverse[None]
        training[c * size : (c + 1) * size] = piece.astype(BF16)
        rows = pl.ds(c * size, size)
        copies.append(pltpu.make_async_copy(training.at[rows], training_hbm.at[rows], sem.at[c + 1]))
        copies[-1].start()
    for copy in copies:
        copy.wait()


def local(elems, params, coords, basis_rows, connectivity, modulus, stiffness):
    own_snaps, modes = coords.shape
    nodes = basis_rows.shape[2]
    count = connectivity.shape[0]
    snaps = own_snaps * params
    ghosts = nodes // 4
    inner = 4 if elems % 4 == 0 else elems
    outer = elems // inner
    half, across = (modes, ghosts) if ghosts % 128 == 0 else (round_up(-(-modes // 2), 32), 2 * ghosts)
    tiles = nodes // 128 + -(-ghosts // 128)
    wide = round_up(modes + 1, 128)
    dma = pltpu.SemaphoreType.DMA
    vmem = pl.BlockSpec(memory_space=pltpu.VMEM)
    hbm = pl.BlockSpec(memory_space=pltpu.HBM)
    dofs = stiffness.shape[0]
    tall = round_up(own_snaps, 8)
    pieces = [
        (stiffness, 0),
        (connectivity.T, dofs),
        (modulus[None], dofs + 8),
        (coords, dofs + 16),
    ]
    height, across_small = dofs + 16 + tall, round_up(max(modes, count), 128)
    small = None
    for piece, at in pieces:
        placed = lax.pad(
            piece, jnp.zeros((), piece.dtype),
            ((at, height - at - piece.shape[0], 0), (0, across_small - piece.shape[1], 0)),
        ).astype(F32)
        small = placed if small is None else small + placed
    cols, flat = pl.pallas_call(
        functools.partial(kernel, elems, params, inner, own_snaps, modes, dofs),
        out_shape=(
            jax.ShapeDtypeStruct((modes * snaps, count), F32),
            jax.ShapeDtypeStruct((snaps, wide), F32),
        ),
        in_specs=[vmem, hbm],
        out_specs=(vmem, vmem),
        scratch_shapes=[
            pltpu.VMEM((modes, 3 * nodes), BF16),
            pltpu.VMEM((3, round_up(half, 16), across), BF16),
            pltpu.VMEM((3, round_up(half, 16), across), BF16),
            pltpu.VMEM((modes, 3 * ghosts), BF16),
            pltpu.VMEM((params, tiles, 3, own_snaps, 128), F32),
            pltpu.VMEM((nodes + ghosts, count), BF16),
            pltpu.VMEM((3 * nodes, 2 * count), BF16),
            pltpu.VMEM((snaps // 2, 3 * ghosts, 2 * count), BF16),
            pltpu.VMEM((snaps // 2, modes, 2 * count), F32),
            pltpu.VMEM((wide, 128), F32),
            pltpu.VMEM((params, snaps, wide), F32),
            pltpu.VMEM((inner, snaps, wide), F32),
            pltpu.VMEM((outer, snaps, wide), F32),
            dma((3,)), dma, dma,
            dma((params,)), dma((params,)),
            dma((params,)), dma((params,)),
            dma((params,)), dma((params,)),
            dma((inner,)), dma((inner,)),
            dma((outer,)), dma((outer,)),
        ],
        compiler_params=pltpu.CompilerParams(
            collective_id=0, has_side_effects=True, vmem_limit_bytes=44 * 1024 * 1024
        ),
    )(small, basis_rows)
    chunks = next(c for c in (4, 3, 2, 1) if modes % c == 0)
    training, target = pl.pallas_call(
        functools.partial(finish_kernel, count * elems * params),
        out_shape=(
            jax.ShapeDtypeStruct((modes, snaps, count), BF16),
            jax.ShapeDtypeStruct((snaps, modes), F32),
        ),
        in_specs=[vmem, vmem],
        out_specs=(hbm, hbm),
        scratch_shapes=[
            pltpu.VMEM((modes, snaps, count), BF16),
            pltpu.VMEM((snaps, modes), F32),
            dma((chunks + 1,)),
        ],
        compiler_params=pltpu.CompilerParams(vmem_limit_bytes=20 * 1024 * 1024),
    )(cols, flat)
    return (jnp.transpose(training, (1, 0, 2)), target)


def solution(mesh):
    in_specs = (
        P("param", None),
        P(None, None, "elem"),
        P(("elem", "param"), None),
        P(("elem", "param")),
        P(),
    )
    out_specs = (P(None, None, ("elem", "param")), P())
    run = functools.partial(local, mesh.shape["elem"], mesh.shape["param"])
    return jax.shard_map(run, mesh=mesh, in_specs=in_specs, out_specs=out_specs, check_vma=False)
```

profile of v0, /device:TPU:0, one launch (start us, length us, event | category | flops | bytes accessed | tf_op | source)
XLA Modules:
  0.0 25.4 jit_solution(11822997968967597844)
XLA Ops:
  0.6 0.7 %convert_add_fusion.small_ref = f32[48,384]{1,0:T(8,128)S(1)} fusion(f32[1,128]{1,0:T(1,128)} %bitcast.4, s32[8,128]{1,0:T(8,128)} %bitcast.3, f32[24,24]{1,0:T(8,128)} %param.9, bf16[4,300]{1,0:T(4,128)(2,1)} %param.5), kind=kLoop, calls=%fused_computation | loop fusion | flops 92160 | bytes 83040 | tf_op jit(solution)/shard_map/add | solution.py:288
  1.4 0.0 copy-start
  1.4 1.0 %copy-done = bf16[3,300,256]{2,1,0:T(8,128)(2,1)S(1)} copy-done((bf16[3,300,256]{2,1,0:T(8,128)(2,1)S(1)}, bf16[3,300,256]{2,1,0:T(8,128)(2,1)}, u32[]{:S(2)}) %copy-start) | copy-done | bytes 460824
  2.4 22.0 %shard_map.68 = (f32[2400,128]{1,0:T(8,128)S(1)}, f32[8,384]{1,0:T(8,128)S(1)}) custom-call(f32[48,384]{1,0:T(8,128)S(1)} %convert_add_fusion.small_ref, bf16[3,300,256]{2,1,0:T(8,128)(2,1)S(1)} %copy-done), custom_call_target="tpu_custom_call" | custom-call | tf_op jit(solution)/shard_map/pallas_call | solution.py:289
  24.4 1.0 %shard_map.69 = (bf16[300,8,128]{2,1,0:T(8,128)(2,1)}, f32[8,300]{1,0:T(8,128)}) custom-call(f32[2400,128]{1,0:T(8,128)S(1)} %get-tuple-element.6.cols_ref, f32[8,384]{1,0:T(8,128)S(1)} %get-tuple-element.7.flat_ref), custom_call_target="tpu_custom_call" | custom-call | tf_op jit(solution)/shard_map/pallas_call | solution.py:323
Async XLA Ops:
  1.4 1.0 %copy-start = (bf16[3,300,256]{2,1,0:T(8,128)(2,1)S(1)}, bf16[3,300,256]{2,1,0:T(8,128)(2,1)}, u32[]{:S(2)}) copy-start(bf16[3,300,256]{2,1,0:T(8,128)(2,1)} %basis_hbm.1) | copy-start | bytes 1382404
where the time goes:
time: 25.6 us; the launch traced here: 25.4 us
  Pallas kernels  22.9 us (89%)
  local copies, waits for them, and re-layouts  1.02 us (4%)
  other arithmetic  0.75 us (3%)
  between operations  0.65 us (3%)
    pallas_call x1, Pallas kernels, local(): pl.pallas_call(functools.partial(kernel, elems, params, inner, own_snaps,...  22 us
    unnamed x2, local copies, waits for them, and re-layouts  1.02 us
    pallas_call x1, Pallas kernels, local(): pl.pallas_call(functools.partial(finish_kernel, count * elems * params),...  0.96 us
    add x1, other arithmetic, local(): small = placed if small is None else small + placed  0.75 us

commit v1 on v0

v1 whole, which is shorter than its diff:
```python
import functools
import math

import jax
import jax.numpy as jnp
from jax import lax
from jax.experimental import pallas as pl
from jax.experimental.pallas import tpu as pltpu
from jax.sharding import PartitionSpec as P

MESH = pl.DeviceIdType.MESH
F32 = jnp.float32
BF16 = jnp.bfloat16
UNROLL = 64


def round_up(value, to):
    return -(-value // to) * to


def repeat(count, body):
    if count <= UNROLL:
        for j in range(count):
            body(j)
    else:
        lax.fori_loop(0, count, lambda j, c: (body(j), c)[1], 0)


def kernel(
    elems, params,
    coords_hbm, basis_hbm, conn_hbm, modulus_hbm, stiff_hbm,
    training_ref, target_ref,
    coords_ref, basis_ref, conn_ref, modulus_ref, stiff_ref,
    cols_ref, packed, ghost_in, ghost, disp, mask, weights, ghost_weights, acc, part,
    norms, part_p, part_e, total_ref,
    load, load_b, send_g, recv_g, send_d, recv_d, send_n, recv_n, send_f, recv_f,
    send_c, recv_c, send_p, recv_p, send_e, recv_e, send_t, recv_t,
):
    own_snaps, modes = coords_hbm.shape
    dofs = stiff_hbm.shape[0]
    snaps = own_snaps * params
    nodes = basis_hbm.shape[2]
    ghosts = nodes // 4
    total_nodes = nodes + ghosts
    count = conn_hbm.shape[1]
    devices = elems * params
    elem_total = count * devices
    me_e, me_p = lax.axis_index("elem"), lax.axis_index("param")
    me = me_e * params + me_p
    lead = params - 1
    before = (me_e + elems - 1) % elems

    def other(j):
        to = (me + j + 1) % devices
        return (to // params, to % params)

    barrier = pltpu.get_barrier_semaphore()
    repeat(devices - 1, lambda j: pl.semaphore_signal(
        barrier, inc=1, device_id=other(j), device_id_type=MESH))

    loads = [
        pltpu.make_async_copy(
            basis_hbm.at[k], basis_ref.at[:, pl.ds(k * nodes, nodes)], load_b.at[k]
        )
        for k in range(3)
    ]
    smalls = [
        pltpu.make_async_copy(src, dst, load.at[i])
        for i, (src, dst) in enumerate([
            (coords_hbm, coords_ref), (conn_hbm, conn_ref),
            (modulus_hbm, modulus_ref), (stiff_hbm, stiff_ref),
        ])
    ]
    for copy in smalls + loads:
        copy.start()

    def remote(src, dst, send, recv, device):
        return pltpu.make_async_remote_copy(
            src_ref=src, dst_ref=dst, send_sem=send, recv_sem=recv,
            device_id=device, device_id_type=MESH,
        )

    own_tiles = nodes // 128
    ghost_tiles = disp.shape[1] - own_tiles
    half = packed.shape[1]
    split = half < modes
    for copy in smalls:
        copy.wait()
    coords = coords_ref[...]
    for k in range(3):
        loads[k].wait()
        moved = jnp.dot(
            coords, basis_ref[:, k * nodes : (k + 1) * nodes], preferred_element_type=F32
        )
        moved = moved.astype(BF16).astype(F32)
        for t in range(own_tiles):
            disp[me_p, t, k] = moved[:, t * 128 : (t + 1) * 128]
    for k in range(3):
        at = k * nodes
        if split:
            packed[k, :, :ghosts] = basis_ref[:half, at : at + ghosts]
            packed[k, : modes - half, ghosts:] = basis_ref[half:, at : at + ghosts]
        else:
            packed[k, :modes] = basis_ref[:, at : at + ghosts]

    pl.semaphore_wait(barrier, devices - 1)
    own_part, ghost_part = pl.ds(0, own_tiles), pl.ds(own_tiles, ghost_tiles)
    sends, arrivals = [], []
    for p in range(params):
        turn = (me_p + p) % params
        source = (me_p + params - p) % params
        sends.append(remote(
            disp.at[me_p, pl.ds(0, ghost_tiles)], disp.at[me_p, ghost_part],
            send_d.at[p], recv_d.at[me_p], (before, turn),
        ))
        arrivals.append(remote(
            disp.at[source, pl.ds(0, ghost_tiles)], disp.at[source, ghost_part],
            send_d.at[p], recv_d.at[source], (before, turn),
        ))
        if p:
            sends.append(remote(
                disp.at[me_p, own_part], disp.at[me_p, own_part],
                send_n.at[p], recv_n.at[me_p], (me_e, turn),
            ))
            arrivals.append(remote(
                disp.at[source, own_part], disp.at[source, own_part],
                send_n.at[p], recv_n.at[source], (me_e, turn),
            ))
    for copy in sends:
        copy.start()
    ghost_copy = remote(packed, ghost_in, send_g, recv_g, (before, lead))
    hand_on = [
        remote(ghost_in, ghost_in, send_f.at[p], recv_f, (me_e, p)) for p in range(params - 1)
    ]

    @pl.when(me_p == lead)
    def _():
        ghost_copy.start()

    corners = conn_ref[...]
    base = jnp.min(corners, axis=0, keepdims=True)
    residue = corners % 8
    lane_at = corners % 128
    tile_at = corners // 128
    node = lax.broadcasted_iota(jnp.int32, (total_nodes, count), 0)
    inside = (node >= base) & (node < base + 8)
    mask[...] = jnp.where(inside, 1.0, 0.0).astype(BF16)
    stiff = stiff_ref[...]
    high = stiff.astype(BF16)
    rest = stiff - high.astype(F32)
    mid = rest.astype(BF16)
    low = (rest - mid.astype(F32)).astype(BF16)
    modulus = modulus_ref[...]
    modulus2 = jnp.concatenate([modulus, modulus], axis=1)
    part[...] = jnp.zeros_like(part)
    lane = lax.broadcasted_iota(jnp.int32, (1, 128), 1)
    row8 = lax.broadcasted_iota(jnp.int32, (8, count), 0)

    for copy in arrivals:
        copy.wait_recv()

    def own_product(p):
        pieces = []
        for at in range(2):
            s = 2 * p + at
            rows = []
            for k in range(3):
                found = jnp.zeros((8, count), F32)
                for t in range(disp.shape[1]):
                    line = disp[s // own_snaps, t, k, pl.ds(s % own_snaps, 1), :]
                    got = jnp.take_along_axis(jnp.broadcast_to(line, (8, 128)), lane_at, axis=1)
                    found = jnp.where(tile_at == t, got, found)
                rows.append(found)
            pieces.append(jnp.concatenate(rows, axis=0))
        moved = jnp.concatenate(pieces, axis=1)
        moved16 = moved.astype(BF16)
        linear = jnp.dot(low, moved16, preferred_element_type=F32)
        linear = linear + jnp.dot(mid, moved16, preferred_element_type=F32)
        linear = linear + jnp.dot(high, moved16, preferred_element_type=F32)
        forces = (modulus2 * (linear + 0.25 * moved * moved * moved)).astype(BF16).astype(F32)
        for at in range(2):
            for k in range(3):
                spread = jnp.zeros((8, count), F32)
                for a in range(8):
                    force = forces[k * 8 + a : k * 8 + a + 1, at * count : (at + 1) * count]
                    spread = spread + jnp.where(residue[a : a + 1] == row8, force, 0.0)
                twice = jnp.concatenate([spread, spread], axis=0).astype(BF16)
                tall = jnp.concatenate([twice] * (total_nodes // 16), axis=0) * mask[...]
                columns = slice(at * count, (at + 1) * count)
                weights[k * nodes : (k + 1) * nodes, columns] = tall[:nodes]
                ghost_weights[p, k * ghosts : (k + 1) * ghosts, columns] = tall[nodes:]
        acc[p] = jnp.dot(basis_ref[...], weights[...], preferred_element_type=F32)

    def whole_product(p, carry):
        sums, squares = carry
        result = acc[p] + jnp.dot(ghost[...], ghost_weights[p], preferred_element_type=F32)
        for at in range(2):
            s = 2 * p + at
            mine = result[:, at * count : (at + 1) * count]
            cols_ref[pl.ds(s, modes, stride=snaps), :] = mine
            norm = jnp.sum(mine * mine, axis=0, keepdims=True)
            squares = jnp.where(row == s, norm, squares)
            sums = jnp.where(lane == s, jnp.sum(mine, axis=1, keepdims=True), sums)
        return sums, squares

    pairs = snaps // 2
    if pairs <= 4:
        for p in range(pairs):
            own_product(p)
    else:
        lax.fori_loop(0, pairs, lambda p, c: (own_product(p), c)[1], 0)

    @pl.when(me_p == lead)
    def _():
        ghost_copy.wait_recv()
        for copy in hand_on:
            copy.start()

    @pl.when(me_p != lead)
    def _():
        remote(ghost_in, ghost_in, send_f.at[0], recv_f, (me_e, lead)).wait_recv()

    for k in range(3):
        if split:
            ghost[:half, k * ghosts : (k + 1) * ghosts] = ghost_in[k, :, :ghosts]
            ghost[half:, k * ghosts : (k + 1) * ghosts] = ghost_in[k, : modes - half, ghosts:]
        else:
            ghost[:, k * ghosts : (k + 1) * ghosts] = ghost_in[k, :modes]
    row = lax.broadcasted_iota(jnp.int32, (snaps, 128), 0)
    across = lax.broadcasted_iota(jnp.int32, (snaps, 128), 1)
    carry = (jnp.zeros((modes, 128), F32), jnp.zeros((snaps, count), F32))
    if pairs <= 4:
        for p in range(pairs):
            carry = whole_product(p, carry)
    else:
        carry = lax.fori_loop(0, pairs, whole_product, carry)
    sums, squares = carry

    norm = jnp.sum(jnp.sqrt(squares), axis=1, keepdims=True)
    norms[me] = jnp.sum(jnp.where(row == across, norm, 0.0), axis=0, keepdims=True)

    def norm_copy(j):
        return remote(norms.at[me], norms.at[me], send_c, recv_c, other(j))

    repeat(devices - 1, lambda j: norm_copy(j).start())

    wide = part_e.shape[2]
    part[:modes] = sums
    flat = jnp.concatenate(
        [jnp.transpose(part[t * 128 : (t + 1) * 128])[:snaps] for t in range(wide // 128)], axis=1
    )
    part_p[me_p] = flat

    def to_lead():
        return remote(part_p.at[me_p], part_p.at[me_p], send_p, recv_p.at[me_p], (me_e, lead))

    def to_elem(j):
        to = (me_e + j + 1) % elems
        return remote(part_e.at[me_e], part_e.at[me_e], send_e.at[j], recv_e.at[me_e], (to, lead))

    def from_elem(j):
        source = (me_e + elems - j - 1) % elems
        return remote(
            part_e.at[source], part_e.at[source], send_e.at[j], recv_e.at[source], (source, lead)
        )

    def result(p):
        return remote(total_ref, total_ref, send_t.at[p], recv_t, (me_e, p))

    @pl.when(me_p != lead)
    def _():
        to_lead().start()

    @pl.when(me_p == lead)
    def _():
        for p in range(params - 1):
            remote(part_p.at[p], part_p.at[p], send_p, recv_p.at[p], (me_e, p)).wait_recv()
        chip = part_p[0]
        for p in range(1, params):
            chip = chip + part_p[p]
        part_e[me_e] = chip
        repeat(elems - 1, lambda j: to_elem(j).start())

    everyone = norms.at[pl.ds(0, devices - 1)]
    gathered = pltpu.make_async_copy(everyone, everyone, recv_c)
    gathered.wait()
    whole = norms[0]
    for d in range(1, devices):
        whole = whole + norms[d]
    diagonal = jnp.where(row == across, jnp.broadcast_to(whole, (snaps, 128)), 0.0)
    row_scale = jnp.sum(diagonal, axis=1, keepdims=True) / elem_total
    inverse = jnp.broadcast_to(1.0 / row_scale, (snaps, count))
    piece = cols_ref[...].reshape(modes, snaps, count) * inverse[None]
    training_ref[...] = piece.astype(BF16)

    @pl.when(me_p == lead)
    def _():
        repeat(elems - 1, lambda j: from_elem(j).wait_recv())
        total = part_e[0]
        for e in range(1, elems):
            total = total + part_e[e]
        total_ref[...] = total
        for p in range(params - 1):
            result(p).start()

    @pl.when(me_p != lead)
    def _():
        remote(total_ref, total_ref, send_t.at[0], recv_t, (me_e, lead)).wait_recv()

    target_ref[...] = total_ref[:, :modes] / (row_scale * math.sqrt(elem_total))

    for copy in sends:
        copy.wait_send()
    pltpu.make_async_copy(everyone, everyone, send_c).wait()

    @pl.when(me_p == lead)
    def _():
        ghost_copy.wait_send()
        for copy in hand_on:
            copy.wait_send()
        repeat(elems - 1, lambda j: to_elem(j).wait_send())
        for p in range(params - 1):
            result(p).wait_send()

    @pl.when(me_p != lead)
    def _():
        to_lead().wait_send()


def finish_kernel(training_ref, target_ref, training_hbm, target_hbm, sem):
    copies = [
        pltpu.make_async_copy(target_ref, target_hbm, sem.at[0]),
        pltpu.make_async_copy(training_ref, training_hbm, sem.at[1]),
    ]
    for copy in copies:
        copy.start()
    for copy in copies:
        copy.wait()


def local(elems, params, coords, basis_rows, connectivity, modulus, stiffness):
    own_snaps, modes = coords.shape
    nodes = basis_rows.shape[2]
    count = connectivity.shape[0]
    snaps = own_snaps * params
    ghosts = nodes // 4
    half, across = (modes, ghosts) if ghosts % 128 == 0 else (round_up(-(-modes // 2), 32), 2 * ghosts)
    tiles = nodes // 128 + -(-ghosts // 128)
    wide = round_up(modes, 128)
    dofs = stiffness.shape[0]
    devices = elems * params
    dma = pltpu.SemaphoreType.DMA
    vmem = pl.BlockSpec(memory_space=pltpu.VMEM)
    hbm = pl.BlockSpec(memory_space=pltpu.HBM)
    training, target = pl.pallas_call(
        functools.partial(kernel, elems, params),
        out_shape=(
            jax.ShapeDtypeStruct((modes, snaps, count), BF16),
            jax.ShapeDtypeStruct((snaps, modes), F32),
        ),
        in_specs=[hbm] * 5,
        out_specs=(vmem, vmem),
        scratch_shapes=[
            pltpu.VMEM((own_snaps, modes), BF16),
            pltpu.VMEM((modes, 3 * nodes), BF16),
            pltpu.VMEM((8, count), jnp.int32),
            pltpu.VMEM((1, count), F32),
            pltpu.VMEM((dofs, dofs), F32),
            pltpu.VMEM((modes * snaps, count), F32),
            pltpu.VMEM((3, round_up(half, 16), across), BF16),
            pltpu.VMEM((3, round_up(half, 16), across), BF16),
            pltpu.VMEM((modes, 3 * ghosts), BF16),
            pltpu.VMEM((params, tiles, 3, own_snaps, 128), F32),
            pltpu.VMEM((nodes + ghosts, count), BF16),
            pltpu.VMEM((3 * nodes, 2 * count), BF16),
            pltpu.VMEM((snaps // 2, 3 * ghosts, 2 * count), BF16),
            pltpu.VMEM((snaps // 2, modes, 2 * count), F32),
            pltpu.VMEM((wide, 128), F32),
            pltpu.VMEM((devices, 1, 128), F32),
            pltpu.VMEM((params, snaps, wide), F32),
            pltpu.VMEM((elems, snaps, wide), F32),
            pltpu.VMEM((snaps, wide), F32),
            dma((4,)), dma((3,)), dma, dma,
            dma((params,)), dma((params,)),
            dma((params,)), dma((params,)),
            dma((params,)), dma,
            dma, dma,
            dma, dma((params,)),
            dma((elems,)), dma((elems,)),
            dma((params,)), dma,
        ],
        compiler_params=pltpu.CompilerParams(
            collective_id=0, has_side_effects=True, vmem_limit_bytes=40 * 1024 * 1024
        ),
    )(*(pltpu.with_memory_space_constraint(x, pltpu.HBM) for x in (
        coords, basis_rows, connectivity.T, modulus[None], stiffness
    )))
    training, target = pl.pallas_call(
        finish_kernel,
        out_shape=(
            jax.ShapeDtypeStruct((modes, snaps, count), BF16),
            jax.ShapeDtypeStruct((snaps, modes), F32),
        ),
        in_specs=[vmem, vmem],
        out_specs=(hbm, hbm),
        scratch_shapes=[dma((2,))],
        compiler_params=pltpu.CompilerParams(vmem_limit_bytes=20 * 1024 * 1024),
    )(training, target)
    return (jnp.transpose(training, (1, 0, 2)), target)


def solution(mesh):
    in_specs = (
        P("param", None),
        P(None, None, "elem"),
        P(("elem", "param"), None),
        P(("elem", "param")),
        P(),
    )
    out_specs = (P(None, None, ("elem", "param")), P())
    run = functools.partial(local, mesh.shape["elem"], mesh.shape["param"])
    return jax.shard_map(run, mesh=mesh, in_specs=in_specs, out_specs=out_specs, check_vma=False)
```

time: 25.6 us -> 22.2 us (0.87)
  Pallas kernels: 22.9 us -> 21.4 us
  local copies, waits for them, and re-layouts: 1.02 us -> 0 us
  other arithmetic: 0.75 us -> 0 us
    pallas_call x2, Pallas kernels: 22.9 us -> 21.4 us  [the longest x1 20.6 us: local(): pl.pallas_call(functools.partial(kernel, elems, params), out_shape=(jax.S...]
    unnamed x2 -> x0, local copies, waits for them, and re-layouts: 1.02 us -> none
    add x1 -> x0, other arithmetic: 0.75 us -> none  [local(): small = placed if small is None else small + placed]
where the time goes in v1:
time: 22.2 us; the launch traced here: 22.1 us
  Pallas kernels  21.4 us (96%)
  between operations  0.64 us (3%)
    pallas_call x1, Pallas kernels, local(): pl.pallas_call(functools.partial(kernel, elems, params), out_shape=(jax.S...  20.6 us
    pallas_call x1, Pallas kernels, local(): pl.pallas_call(finish_kernel, out_shape=(jax.ShapeDtypeStruct((modes, sna...  0.85 us

profile of v1, /device:TPU:0, one launch (start us, length us, event | category | flops | bytes accessed | tf_op | source)
XLA Modules:
  0.0 22.1 jit_solution(2986168399101445626)
XLA Ops:
  0.6 20.6 %shard_map.68 = (bf16[300,8,128]{2,1,0:T(8,128)(2,1)S(1)}, f32[8,300]{1,0:T(8,128)S(1)}) custom-call(bf16[4,300]{1,0:T(4,128)(2,1)} %coords_hbm.1, bf16[3,300,256]{2,1,0:T(8,128)(2,1)} %basis_hbm.1, s32[8,128]{1,0:T(8,128)} %bitcast.3, f32[1,128]{1,0:T(1,128)} %bitcast.4, f32[24,24]{1,0:T(8,128)} %stiff_hbm.1), custom_call_target="tpu_custom_call" | custom-call | tf_op jit(solution)/shard_map/pallas_call | solution.py:355
  21.2 0.8 %shard_map.69 = (bf16[300,8,128]{2,1,0:T(8,128)(2,1)}, f32[8,300]{1,0:T(8,128)}) custom-call(bf16[300,8,128]{2,1,0:T(8,128)(2,1)S(1)} %get-tuple-element.6.training_ref, f32[8,300]{1,0:T(8,128)S(1)} %get-tuple-element.7.target_ref), custom_call_target="tpu_custom_call" | custom-call | tf_op jit(solution)/shard_map/pallas_call | solution.py:398

commit v2 on v1

--- a/solution.py
+++ b/solution.py
@@ -8,7 +8,7 @@
 from jax.experimental.pallas import tpu as pltpu
 from jax.sharding import PartitionSpec as P
 
-MESH = pl.DeviceIdType.MESH
+LOGICAL = pl.DeviceIdType.LOGICAL
 F32 = jnp.float32
 BF16 = jnp.bfloat16
 UNROLL = 64
@@ -27,14 +27,15 @@
 
 
 def kernel(
-    elems, params,
+    elems, params, inner,
     coords_hbm, basis_hbm, conn_hbm, modulus_hbm, stiff_hbm,
     training_ref, target_ref,
     coords_ref, basis_ref, conn_ref, modulus_ref, stiff_ref,
     cols_ref, packed, ghost_in, ghost, disp, mask, weights, ghost_weights, acc, part,
-    norms, part_p, part_e, total_ref,
+    norms, part_p, part_e, total_ref, relay_disp, relay_ghost,
     load, load_b, send_g, recv_g, send_d, recv_d, send_n, recv_n, send_f, recv_f,
     send_c, recv_c, send_p, recv_p, send_e, recv_e, send_t, recv_t,
+    send_rd, recv_rd, send_rg, recv_rg, known,
 ):
     own_snaps, modes = coords_hbm.shape
     dofs = stiff_hbm.shape[0]
@@ -48,15 +49,28 @@
     me_e, me_p = lax.axis_index("elem"), lax.axis_index("param")
     me = me_e * params + me_p
     lead = params - 1
-    before = (me_e + elems - 1) % elems
+    first, last = me_e == 0, me_e == elems - 1
+    before = jnp.where(first, elems - 1, me_e - 1)
+    relay_e = elems // 4
+    relay = relay_e * params + lead
+    relaying = me == relay
+    me_o = lax.div(me_e, inner)
+    bottom, top = me_o == 0, me_o == elems // inner - 1
+
+    def dev(e, p):
+        return e * params + p
 
     def other(j):
-        to = (me + j + 1) % devices
-        return (to // params, to % params)
-
-    barrier = pltpu.get_barrier_semaphore()
-    repeat(devices - 1, lambda j: pl.semaphore_signal(
-        barrier, inc=1, device_id=other(j), device_id_type=MESH))
+        to = me + (j + 1)
+        return jnp.where(to >= devices, to - devices, to)
+
+    def flipped(index, stride):
+        return jnp.where(lax.rem(lax.div(index, stride), 2) == 0, index + stride, index - stride)
+
+    strides = [2**b for b in range(params.bit_length() - 1)]
+    flips = [dev(me_e, flipped(me_p, stride)) for stride in strides]
+    strides = [2**b for b in range(inner.bit_length() - 1)]
+    flips += [dev(flipped(me_e, stride), me_p) for stride in strides]
 
     loads = [
         pltpu.make_async_copy(
@@ -71,13 +85,54 @@
             (modulus_hbm, modulus_ref), (stiff_hbm, stiff_ref),
         ])
     ]
-    for copy in smalls + loads:
+    for copy in loads + smalls:
         copy.start()
+
+    barrier = pltpu.get_barrier_semaphore()
+
+    def greet(device):
+        pl.semaphore_signal(barrier, inc=1, device_id=device, device_id_type=LOGICAL)
+
+    @pl.when(last | first)
+    def _():
+        greet(relay)
+
+    @pl.when(relaying)
+    def _():
+        for p in range(params):
+            greet(dev(elems - 1, p))
+            greet(dev(0, p))
+
+    @pl.when(jnp.logical_not(first))
+    def _():
+        for p in range(params):
+            greet(dev(me_e - 1, p))
+
+    @pl.when(jnp.logical_not(last))
+    def _():
+        for p in range(params):
+            greet(dev(me_e + 1, p))
+
+    @pl.when(jnp.logical_not(bottom))
+    def _():
+        greet(dev(me_e - inner, me_p))
+
+    @pl.when(jnp.logical_not(top))
+    def _():
+        greet(dev(me_e + inner, me_p))
+
+    for j in range(1, params):
+        greet(dev(me_e, lax.rem(me_p + j, params)))
+    for device in flips:
+        greet(device)
+    greeted = len(flips) + params - 1 + 2 * params + 2
+    greeted += jnp.where(first | last, 1 - params, 0) + jnp.where(relaying, 2 * params, 0)
+    greeted -= jnp.where(bottom | top, 1, 0)
 
     def remote(src, dst, send, recv, device):
         return pltpu.make_async_remote_copy(
             src_ref=src, dst_ref=dst, send_sem=send, recv_sem=recv,
-            device_id=device, device_id_type=MESH,
+            device_id=device, device_id_type=LOGICAL,
         )
 
     own_tiles = nodes // 128
@@ -103,39 +158,70 @@
         else:
             packed[k, :modes] = basis_ref[:, at : at + ghosts]
 
-    pl.semaphore_wait(barrier, devices - 1)
+    pl.semaphore_wait(barrier, greeted)
     own_part, ghost_part = pl.ds(0, own_tiles), pl.ds(own_tiles, ghost_tiles)
-    sends, arrivals = [], []
-    for p in range(params):
-        turn = (me_p + p) % params
-        source = (me_p + params - p) % params
-        sends.append(remote(
-            disp.at[me_p, pl.ds(0, ghost_tiles)], disp.at[me_p, ghost_part],
-            send_d.at[p], recv_d.at[me_p], (before, turn),
-        ))
-        arrivals.append(remote(
-            disp.at[source, pl.ds(0, ghost_tiles)], disp.at[source, ghost_part],
-            send_d.at[p], recv_d.at[source], (before, turn),
-        ))
-        if p:
-            sends.append(remote(
-                disp.at[me_p, own_part], disp.at[me_p, own_part],
-                send_n.at[p], recv_n.at[me_p], (me_e, turn),
-            ))
-            arrivals.append(remote(
-                disp.at[source, own_part], disp.at[source, own_part],
-                send_n.at[p], recv_n.at[source], (me_e, turn),
-            ))
-    for copy in sends:
-        copy.start()
-    ghost_copy = remote(packed, ghost_in, send_g, recv_g, (before, lead))
-    hand_on = [
-        remote(ghost_in, ghost_in, send_f.at[p], recv_f, (me_e, p)) for p in range(params - 1)
-    ]
-
-    @pl.when(me_p == lead)
-    def _():
-        ghost_copy.start()
+    front = disp.at[me_p, pl.ds(0, ghost_tiles)]
+    back = [disp.at[p, ghost_part] for p in range(params)]
+    mine_back = disp.at[me_p, ghost_part]
+
+    def ghost_disp(p):
+        turn = lax.rem(me_p + p, params)
+        return remote(front, mine_back, send_d.at[p], recv_d.at[me_p], dev(before, turn))
+
+    def own_disp(p):
+        turn = lax.rem(me_p + p, params)
+        mine = disp.at[me_p, own_part]
+        return remote(mine, mine, send_n.at[p], recv_n.at[me_p], dev(me_e, turn))
+
+    def to_relay():
+        return remote(front, relay_disp.at[me_p], send_d.at[0], recv_rd.at[me_p], relay)
+
+    def from_relay(q, p):
+        return remote(
+            relay_disp.at[q], back[q], send_rd.at[q * params + p], recv_d.at[q], dev(elems - 1, p)
+        )
+
+    def ghost_copy():
+        return remote(packed, ghost_in, send_g, recv_g, dev(before, lead))
+
+    def ghost_to_relay():
+        return remote(packed, relay_ghost, send_g, recv_rg, relay)
+
+    def ghost_from_relay():
+        return remote(relay_ghost, ghost_in, send_rg, recv_g, dev(elems - 1, lead))
+
+    def hand_on(p):
+        return remote(ghost_in, ghost_in, send_f.at[p], recv_f, dev(me_e, p))
+
+    @pl.when(first)
+    def _():
+        to_relay().start()
+
+    @pl.when(jnp.logical_not(first))
+    def _():
+        for p in range(params):
+            ghost_disp(p).start()
+
+    @pl.when(first & (me_p == lead))
+    def _():
+        ghost_to_relay().start()
+
+    @pl.when(jnp.logical_not(first) & (me_p == lead))
+    def _():
+        ghost_copy().start()
+
+    for p in range(1, params):
+        own_disp(p).start()
+
+    @pl.when(relaying)
+    def _():
+        for q in range(params):
+            remote(front, relay_disp.at[q], send_d.at[0], recv_rd.at[q], relay).wait_recv()
+        for q in range(params):
+            for p in range(params):
+                from_relay(q, params - 1 - p).start()
+        ghost_to_relay().wait_recv()
+        ghost_from_relay().start()
 
     corners = conn_ref[...]
     base = jnp.min(corners, axis=0, keepdims=True)
@@ -156,8 +242,33 @@
     lane = lax.broadcasted_iota(jnp.int32, (1, 128), 1)
     row8 = lax.broadcasted_iota(jnp.int32, (8, count), 0)
 
-    for copy in arrivals:
-        copy.wait_recv()
+    def tell(at, device):
+        pl.semaphore_signal(known.at[at], inc=1, device_id=device, device_id_type=LOGICAL)
+
+    for at, device in enumerate(flips):
+        tell(at, device)
+        pl.semaphore_wait(known.at[at], 1)
+    up, down = len(flips), len(flips) + 1
+
+    @pl.when(jnp.logical_not(bottom))
+    def _():
+        pl.semaphore_wait(known.at[up], 1)
+
+    @pl.when(jnp.logical_not(top))
+    def _():
+        tell(up, dev(me_e + inner, me_p))
+        pl.semaphore_wait(known.at[down], 1)
+
+    @pl.when(jnp.logical_not(bottom))
+    def _():
+        tell(down, dev(me_e - inner, me_p))
+
+    for q in range(params):
+        remote(front, back[q], send_d.at[0], recv_d.at[q], me).wait_recv()
+    for j in range(1, params):
+        q = lax.rem(me_p + j, params)
+        own = disp.at[q, own_part]
+        remote(own, own, send_n.at[0], recv_n.at[q], me).wait_recv()
 
     def own_product(p):
         pieces = []
@@ -212,13 +323,13 @@
 
     @pl.when(me_p == lead)
     def _():
-        ghost_copy.wait_recv()
-        for copy in hand_on:
-            copy.start()
+        ghost_copy().wait_recv()
+        for p in range(params - 1):
+            hand_on(p).start()
 
     @pl.when(me_p != lead)
     def _():
-        remote(ghost_in, ghost_in, send_f.at[0], recv_f, (me_e, lead)).wait_recv()
+        hand_on(0).wait_recv()
 
     for k in range(3):
         if split:
@@ -252,20 +363,23 @@
     part_p[me_p] = flat
 
     def to_lead():
-        return remote(part_p.at[me_p], part_p.at[me_p], send_p, recv_p.at[me_p], (me_e, lead))
+        return remote(part_p.at[me_p], part_p.at[me_p], send_p, recv_p.at[me_p], dev(me_e, lead))
+
+    def wrapped(e):
+        return jnp.where(e >= elems, e - elems, e)
 
     def to_elem(j):
-        to = (me_e + j + 1) % elems
-        return remote(part_e.at[me_e], part_e.at[me_e], send_e.at[j], recv_e.at[me_e], (to, lead))
+        to = wrapped(me_e + (j + 1))
+        return remote(part_e.at[me_e], part_e.at[me_e], send_e.at[j], recv_e.at[me_e], dev(to, lead))
 
     def from_elem(j):
-        source = (me_e + elems - j - 1) % elems
+        source = wrapped(me_e + elems - j - 1)
         return remote(
-            part_e.at[source], part_e.at[source], send_e.at[j], recv_e.at[source], (source, lead)
+            part_e.at[source], part_e.at[source], send_e.at[j], recv_e.at[source], dev(source, lead)
         )
 
     def result(p):
-        return remote(total_ref, total_ref, send_t.at[p], recv_t, (me_e, p))
+        return remote(total_ref, total_ref, send_t.at[p], recv_t, dev(me_e, p))
 
     @pl.when(me_p != lead)
     def _():
@@ -274,7 +388,7 @@
     @pl.when(me_p == lead)
     def _():
         for p in range(params - 1):
-            remote(part_p.at[p], part_p.at[p], send_p, recv_p.at[p], (me_e, p)).wait_recv()
+            remote(part_p.at[p], part_p.at[p], send_p, recv_p.at[p], me).wait_recv()
         chip = part_p[0]
         for p in range(1, params):
             chip = chip + part_p[p]
@@ -305,19 +419,35 @@
 
     @pl.when(me_p != lead)
     def _():
-        remote(total_ref, total_ref, send_t.at[0], recv_t, (me_e, lead)).wait_recv()
+        result(0).wait_recv()
 
     target_ref[...] = total_ref[:, :modes] / (row_scale * math.sqrt(elem_total))
 
-    for copy in sends:
-        copy.wait_send()
+    for p in range(1, params):
+        own_disp(p).wait_send()
     pltpu.make_async_copy(everyone, everyone, send_c).wait()
 
+    @pl.when(first)
+    def _():
+        to_relay().wait_send()
+
+    @pl.when(jnp.logical_not(first))
+    def _():
+        for p in range(params):
+            ghost_disp(p).wait_send()
+
+    @pl.when(relaying)
+    def _():
+        for q in range(params):
+            for p in range(params):
+                from_relay(q, p).wait_send()
+        ghost_from_relay().wait_send()
+
     @pl.when(me_p == lead)
     def _():
-        ghost_copy.wait_send()
-        for copy in hand_on:
-            copy.wait_send()
+        ghost_copy().wait_send()
+        for p in range(params - 1):
+            hand_on(p).wait_send()
         repeat(elems - 1, lambda j: to_elem(j).wait_send())
         for p in range(params - 1):
             result(p).wait_send()
@@ -349,11 +479,13 @@
     wide = round_up(modes, 128)
     dofs = stiffness.shape[0]
     devices = elems * params
+    inner = 4
+    rounds = params.bit_length() + inner.bit_length() - 2
     dma = pltpu.SemaphoreType.DMA
     vmem = pl.BlockSpec(memory_space=pltpu.VMEM)
     hbm = pl.BlockSpec(memory_space=pltpu.HBM)
     training, target = pl.pallas_call(
-        functools.partial(kernel, elems, params),
+        functools.partial(kernel, elems, params, inner),
         out_shape=(
             jax.ShapeDtypeStruct((modes, snaps, count), BF16),
             jax.ShapeDtypeStruct((snaps, modes), F32),
@@ -380,6 +512,8 @@
             pltpu.VMEM((params, snaps, wide), F32),
             pltpu.VMEM((elems, snaps, wide), F32),
             pltpu.VMEM((snaps, wide), F32),
+            pltpu.VMEM((params, tiles - nodes // 128, 3, own_snaps, 128), F32),
+            pltpu.VMEM((3, round_up(half, 16), across), BF16),
             dma((4,)), dma((3,)), dma, dma,
             dma((params,)), dma((params,)),
             dma((params,)), dma((params,)),
@@ -388,6 +522,8 @@
             dma, dma((params,)),
             dma((elems,)), dma((elems,)),
             dma((params,)), dma,
+            dma((params * params,)), dma((params,)), dma, dma,
+            pltpu.SemaphoreType.REGULAR((rounds + 2,)),
         ],
         compiler_params=pltpu.CompilerParams(
             collective_id=0, has_side_effects=True, vmem_limit_bytes=40 * 1024 * 1024

time: 22.2 us -> 22.4 us (level)
  no operation moved by 1% of the time
where the time goes in v2:
time: 22.4 us; the launch traced here: 22.2 us
  Pallas kernels  21.6 us (96%)
  between operations  0.64 us (3%)
    pallas_call x1, Pallas kernels, local(): pl.pallas_call(functools.partial(kernel, elems, params, inner), out_shape...  20.7 us
    pallas_call x1, Pallas kernels, local(): pl.pallas_call(finish_kernel, out_shape=(jax.ShapeDtypeStruct((modes, sna...  0.85 us

profile of v2, /device:TPU:0, one launch (start us, length us, event | category | flops | bytes accessed | tf_op | source)
XLA Modules:
  0.0 22.2 jit_solution(7391186029763254414)
XLA Ops:
  0.6 20.7 %shard_map.68 = (bf16[300,8,128]{2,1,0:T(8,128)(2,1)S(1)}, f32[8,300]{1,0:T(8,128)S(1)}) custom-call(bf16[4,300]{1,0:T(4,128)(2,1)} %coords_hbm.1, bf16[3,300,256]{2,1,0:T(8,128)(2,1)} %basis_hbm.1, s32[8,128]{1,0:T(8,128)} %bitcast.3, f32[1,128]{1,0:T(1,128)} %bitcast.4, f32[24,24]{1,0:T(8,128)} %stiff_hbm.1), custom_call_target="tpu_custom_call" | custom-call | tf_op jit(solution)/shard_map/pallas_call | solution.py:487
  21.4 0.8 %shard_map.69 = (bf16[300,8,128]{2,1,0:T(8,128)(2,1)}, f32[8,300]{1,0:T(8,128)}) custom-call(bf16[300,8,128]{2,1,0:T(8,128)(2,1)S(1)} %get-tuple-element.6.training_ref, f32[8,300]{1,0:T(8,128)S(1)} %get-tuple-element.7.target_ref), custom_call_target="tpu_custom_call" | custom-call | tf_op jit(solution)/shard_map/pallas_call | solution.py:534

commit v3 on v2

v3 whole, which is shorter than its diff:
```python
import functools
import math

import jax
import jax.numpy as jnp
from jax import lax
from jax.experimental import pallas as pl
from jax.experimental.pallas import tpu as pltpu
from jax.sharding import PartitionSpec as P

LOGICAL = pl.DeviceIdType.LOGICAL
F32 = jnp.float32
BF16 = jnp.bfloat16
UNROLL = 64


def round_up(value, to):
    return -(-value // to) * to


def repeat(count, body):
    if count <= UNROLL:
        for j in range(count):
            body(j)
    else:
        lax.fori_loop(0, count, lambda j, c: (body(j), c)[1], 0)


def kernel(
    elems, params, inner,
    coords_hbm, basis_hbm, conn_hbm, modulus_hbm, stiff_hbm,
    training_ref, target_ref,
    coords_ref, basis_ref, conn_ref, modulus_ref, stiff_ref,
    packed, ghost_in, ghost, disp, corner_disp, weights, edge_weights, acc, cols_ref, part, nodal,
    norms, part_p, part_e, total_ref, relay_disp, relay_ghost,
    load, load_b, send_g, recv_g, send_d, recv_d, send_n, recv_n, send_f, recv_f,
    send_c, recv_c, send_p, recv_p, send_e, recv_e, send_t, recv_t,
    send_rd, recv_rd, send_rg, recv_rg, climb, known,
):
    own_snaps, modes = coords_hbm.shape
    dofs = stiff_hbm.shape[0]
    snaps = own_snaps * params
    pairs = snaps // 2
    nodes = basis_hbm.shape[2]
    ghosts = nodes // 4
    count = conn_hbm.shape[1]
    devices = elems * params
    outer = elems // inner
    elem_total = count * devices
    wide, edge = part_e.shape[2], ghost.shape[1]
    own_tiles = nodes // 128
    ghost_tiles = disp.shape[1] - own_tiles
    me_e, me_p = lax.axis_index("elem"), lax.axis_index("param")
    me = me_e * params + me_p
    lead = params - 1
    leading = me_p == lead
    first, last = me_e == 0, me_e == elems - 1
    before = jnp.where(first, elems - 1, me_e - 1)
    relay = elems // 4 * params + lead
    relaying = me == relay
    me_o, me_i = lax.div(me_e, inner), lax.rem(me_e, inner)
    bottom, top = me_o == 0, me_o == outer - 1
    climbing = me_p == 0

    def dev(e, p):
        return e * params + p

    def other(j):
        to = me + (j + 1)
        return jnp.where(to >= devices, to - devices, to)

    def signal(semaphore, device):
        pl.semaphore_signal(semaphore, inc=1, device_id=device, device_id_type=LOGICAL)

    def remote(src, dst, send, recv, device):
        return pltpu.make_async_remote_copy(
            src_ref=src, dst_ref=dst, send_sem=send, recv_sem=recv,
            device_id=device, device_id_type=LOGICAL,
        )

    def wait_bytes(ref, semaphore):
        pltpu.make_async_copy(ref, ref, semaphore).wait()

    load_basis = pltpu.make_async_copy(basis_hbm, basis_ref, load_b)
    smalls = [
        pltpu.make_async_copy(src, dst, load.at[i])
        for i, (src, dst) in enumerate([
            (coords_hbm, coords_ref), (conn_hbm, conn_ref),
            (modulus_hbm, modulus_ref), (stiff_hbm, stiff_ref),
        ])
    ]
    for copy in [load_basis] + smalls:
        copy.start()

    barrier = pltpu.get_barrier_semaphore()
    below = jnp.logical_not(first) & (me_i == 0)
    above = jnp.logical_not(last) & (me_i == inner - 1)

    @pl.when(first | last)
    def _():
        signal(barrier, relay)

    @pl.when(relaying)
    def _():
        for p in range(params):
            signal(barrier, dev(elems - 1, p))
            signal(barrier, dev(0, p))

    @pl.when(below)
    def _():
        for p in range(params):
            signal(barrier, dev(me_e - 1, p))

    @pl.when(above)
    def _():
        for p in range(params):
            signal(barrier, dev(me_e + 1, p))

    @pl.when(climbing & jnp.logical_not(bottom))
    def _():
        signal(barrier, dev(me_e - inner, 0))

    @pl.when(climbing & jnp.logical_not(top))
    def _():
        signal(barrier, dev(me_e + inner, 0))

    plane = inner * params
    place = me_i * params + me_p
    for j in range(1, plane):
        to = place + j
        signal(barrier, me_o * plane + jnp.where(to >= plane, to - plane, to))
    greeted = plane - 1 + jnp.where(first | last, 1, 0) + jnp.where(relaying, 2 * params, 0)
    greeted += jnp.where(below, params, 0) + jnp.where(above, params, 0)
    greeted += jnp.where(climbing & jnp.logical_not(bottom), 1, 0)
    greeted += jnp.where(climbing & jnp.logical_not(top), 1, 0)

    part[...] = jnp.zeros_like(part)
    nodal[...] = jnp.zeros_like(nodal)
    tail_at = 3 * ghosts
    for p in range(pairs):
        edge_weights[p, tail_at:] = jnp.zeros((edge - tail_at, 2 * count), BF16)
    for copy in smalls:
        copy.wait()
    coords = coords_ref[...]
    load_basis.wait()
    for k in range(3):
        moved = jnp.dot(coords, basis_ref[k], preferred_element_type=F32)
        moved = moved.astype(BF16).astype(F32)
        for t in range(own_tiles):
            disp[me_p, t, k] = moved[:, t * 128 : (t + 1) * 128]
    rows = packed.shape[0]
    if ghosts % 128 == 0:
        for k in range(3):
            packed[:modes, k * ghosts : (k + 1) * ghosts] = basis_ref[k, :, :ghosts]
    else:
        half = rows - round_up(modes, 16)
        packed[:modes, :ghosts] = basis_ref[0, :, :ghosts]
        packed[:modes, ghosts:] = basis_ref[1, :, :ghosts]
        packed[rows - half :, :ghosts] = basis_ref[2, :half, :ghosts]
        packed[rows - half : rows - 2 * half + modes, ghosts:] = basis_ref[2, half:, :ghosts]

    pl.semaphore_wait(barrier, greeted)
    own_part, ghost_part = pl.ds(0, own_tiles), pl.ds(own_tiles, ghost_tiles)
    front = disp.at[me_p, pl.ds(0, ghost_tiles)]
    backs = disp.at[:, ghost_part]

    def ghost_disp(p):
        turn = lax.rem(me_p + p, params)
        return remote(front, disp.at[me_p, ghost_part], send_d, recv_d, dev(before, turn))

    def own_disp(p):
        turn = lax.rem(me_p + p, params)
        mine = disp.at[me_p, own_part]
        return remote(mine, mine, send_n, recv_n, dev(me_e, turn))

    def to_relay():
        return remote(front, relay_disp.at[me_p], send_d, recv_rd, relay)

    def from_relay(q, p):
        return remote(
            relay_disp.at[q], disp.at[q, ghost_part], send_rd.at[q], recv_d, dev(elems - 1, p)
        )

    def ghost_copy():
        return remote(packed, ghost_in, send_g, recv_g, dev(before, lead))

    def ghost_to_relay():
        return remote(packed, relay_ghost, send_g, recv_rg, relay)

    def ghost_from_relay():
        return remote(relay_ghost, ghost_in, send_rg, recv_g, dev(elems - 1, lead))

    def hand_on(p):
        return remote(ghost_in, ghost_in, send_f.at[p], recv_f, dev(me_e, p))

    @pl.when(first)
    def _():
        to_relay().start()

    @pl.when(jnp.logical_not(first))
    def _():
        for p in range(params):
            ghost_disp(p).start()

    @pl.when(first & leading)
    def _():
        ghost_to_relay().start()

    @pl.when(jnp.logical_not(first) & leading)
    def _():
        ghost_copy().start()

    for p in range(1, params):
        own_disp(p).start()

    @pl.when(relaying)
    def _():
        wait_bytes(relay_disp, recv_rd)
        for q in range(params):
            for p in range(params):
                from_relay(q, params - 1 - p).start()
        ghost_to_relay().wait_recv()
        ghost_from_relay().start()

    @pl.when(climbing & jnp.logical_not(bottom))
    def _():
        pl.semaphore_wait(climb, 1)

    @pl.when(climbing & jnp.logical_not(top))
    def _():
        signal(climb, dev(me_e + inner, 0))

    @pl.when(climbing & top)
    def _():
        for p in range(1, params):
            signal(known, dev(me_e, p))
        for o in range(outer - 1):
            for p in range(params):
                signal(known, dev(o * inner + me_i, p))

    corners = conn_ref[...]
    base = jnp.min(corners, axis=0, keepdims=True)
    residue = corners % 8
    lane_at = corners % 128
    tile_at = corners // 128
    row8 = lax.broadcasted_iota(jnp.int32, (8, count), 0)
    lane = lax.broadcasted_iota(jnp.int32, (1, 128), 1)
    hits = [residue[a : a + 1] == row8 for a in range(8)]

    def inside(start, height):
        node = start + lax.broadcasted_iota(jnp.int32, (height, count), 0)
        return (node >= base) & (node < base + 8)

    own_rows = lax.broadcasted_iota(jnp.int32, (nodes, count), 0) < nodes - 8
    own_mask = jnp.where(inside(0, nodes) & own_rows, 1.0, 0.0).astype(BF16)
    ghost_mask = jnp.where(inside(nodes, ghosts), 1.0, 0.0)
    tail_mask = jnp.where(inside(nodes - 8, 8), 1.0, 0.0)
    stiff = stiff_ref[...]
    high = stiff.astype(BF16)
    rest = stiff - high.astype(F32)
    mid = rest.astype(BF16)
    low = (rest - mid.astype(F32)).astype(BF16)
    modulus = modulus_ref[...]
    modulus2 = jnp.concatenate([modulus, modulus], axis=1)
    tails = [basis_ref[k, :, nodes - 8 :] for k in range(3)]
    start = tail_at // 128 * 128
    blank = [jnp.zeros((modes, tail_at - start), BF16)] if tail_at > start else []
    after = [jnp.zeros((modes, edge - tail_at - 24), BF16)]
    ghost[:, start:] = jnp.concatenate(blank + tails + after, axis=1)

    def gathered(p, found, tiles):
        pieces = []
        for at in range(2):
            s = 2 * p + at
            parts = []
            for k in range(3):
                piece = found[k * 8 : (k + 1) * 8, at * count : (at + 1) * count]
                for t in tiles:
                    line = disp[s // own_snaps, t, k, pl.ds(s % own_snaps, 1), :]
                    got = jnp.take_along_axis(jnp.broadcast_to(line, (8, 128)), lane_at, axis=1)
                    piece = jnp.where(tile_at == t, got, piece)
                parts.append(piece)
            pieces.append(jnp.concatenate(parts, axis=0))
        return jnp.concatenate(pieces, axis=1)

    def forces_of(moved):
        moved16 = moved.astype(BF16)
        linear = jnp.dot(low, moved16, preferred_element_type=F32)
        linear = linear + jnp.dot(mid, moved16, preferred_element_type=F32)
        linear = linear + jnp.dot(high, moved16, preferred_element_type=F32)
        return (modulus2 * (linear + 0.25 * moved * moved * moved)).astype(BF16).astype(F32)

    def spread_of(forces, at, k):
        spread = jnp.zeros((8, count), F32)
        for a in range(8):
            force = forces[k * 8 + a : k * 8 + a + 1, at * count : (at + 1) * count]
            spread = spread + jnp.where(hits[a], force, 0.0)
        return spread.astype(BF16).astype(F32)

    def own_product(p):
        slot = p if weights.shape[0] > 1 else 0
        moved = gathered(p, jnp.zeros((dofs, 2 * count), F32), range(own_tiles))
        corner_disp[p] = moved
        forces = forces_of(moved)
        for at in range(2):
            columns = slice(at * count, (at + 1) * count)
            for k in range(3):
                spread = spread_of(forces, at, k)
                twice = jnp.concatenate([spread, spread], axis=0).astype(BF16)
                tall = jnp.concatenate([twice] * (nodes // 16), axis=0) * own_mask
                weights[slot, k * nodes : (k + 1) * nodes, columns] = tall
        total = jnp.dot(basis_ref[0], weights[slot, :nodes], preferred_element_type=F32)
        for k in range(1, 3):
            total = total + jnp.dot(
                basis_ref[k], weights[slot, k * nodes : (k + 1) * nodes], preferred_element_type=F32
            )
        acc[p] = total

    def own_sums(p):
        for at in range(2):
            mine = acc[p, :, at * count : (at + 1) * count]
            total = jnp.sum(mine, axis=1, keepdims=True)
            part[:modes] = jnp.where(lane == 2 * p + at, total, part[:modes])

    def edge_forces(p):
        moved = gathered(p, corner_disp[p], range(own_tiles, own_tiles + ghost_tiles))
        forces = forces_of(moved)
        for at in range(2):
            columns = slice(at * count, (at + 1) * count)
            ends = []
            for k in range(3):
                spread = spread_of(forces, at, k)
                tall = jnp.concatenate([spread] * (ghosts // 8), axis=0) * ghost_mask
                edge_weights[p, k * ghosts : (k + 1) * ghosts, columns] = tall.astype(BF16)
                ends.append(spread * tail_mask)
                total = jnp.sum(tall, axis=1, keepdims=True)
                at_rows = slice(k * ghosts, (k + 1) * ghosts)
                nodal[at_rows] = jnp.where(lane == 2 * p + at, total, nodal[at_rows])
            end = jnp.concatenate(ends + [jnp.zeros((8, count), F32)], axis=0)
            edge_weights[p, tail_at : tail_at + 32, columns] = end.astype(BF16)
            total = jnp.sum(end, axis=1, keepdims=True)
            at_rows = slice(tail_at, tail_at + 32)
            nodal[at_rows] = jnp.where(lane == 2 * p + at, total, nodal[at_rows])

    def whole_product(p, squares):
        result = acc[p] + jnp.dot(ghost[...], edge_weights[p], preferred_element_type=F32)
        for at in range(2):
            s = 2 * p + at
            mine = result[:, at * count : (at + 1) * count]
            cols_ref[pl.ds(s, modes, stride=snaps), :] = mine
            norm = jnp.sum(mine * mine, axis=0, keepdims=True)
            squares = jnp.where(row == s, norm, squares)
        return squares

    def each_pair(body):
        if pairs <= 4:
            for p in range(pairs):
                body(p)
        else:
            lax.fori_loop(0, pairs, lambda p, c: (body(p), c)[1], 0)

    others = disp.at[pl.ds(0, params - 1), own_part]
    wait_bytes(others, recv_n)
    each_pair(own_product)
    each_pair(own_sums)

    def flipped(ref):
        return jnp.concatenate(
            [jnp.transpose(ref[t * 128 : (t + 1) * 128])[:snaps] for t in range(ref.shape[0] // 128)],
            axis=1,
        )

    part_p[me_p, :, :wide] = flipped(part)
    wait_bytes(backs, recv_d)
    each_pair(edge_forces)
    part_p[me_p, :, wide:] = flipped(nodal)

    def to_lead():
        return remote(part_p.at[me_p], part_p.at[me_p], send_p, recv_p, dev(me_e, lead))

    @pl.when(jnp.logical_not(leading))
    def _():
        to_lead().start()

    @pl.when(leading)
    def _():
        ghost_copy().wait_recv()
        for p in range(params - 1):
            hand_on(p).start()

    @pl.when(jnp.logical_not(leading))
    def _():
        hand_on(0).wait_recv()

    if ghosts % 128 == 0:
        ghost[:, :tail_at] = ghost_in[:modes]
    else:
        ghost[:, : 2 * ghosts] = ghost_in[:modes]
        ghost[:half, 2 * ghosts : tail_at] = ghost_in[rows - half :, :ghosts]
        ghost[half:, 2 * ghosts : tail_at] = ghost_in[rows - half : rows - 2 * half + modes, ghosts:]
    row = lax.broadcasted_iota(jnp.int32, (snaps, 128), 0)
    across = lax.broadcasted_iota(jnp.int32, (snaps, 128), 1)
    squares = jnp.zeros((snaps, count), F32)
    if pairs <= 4:
        for p in range(pairs):
            squares = whole_product(p, squares)
    else:
        squares = lax.fori_loop(0, pairs, whole_product, squares)

    norm = jnp.sum(jnp.sqrt(squares), axis=1, keepdims=True)
    norms[me] = jnp.sum(jnp.where(row == across, norm, 0.0), axis=0, keepdims=True)

    @pl.when(jnp.logical_not(climbing & top))
    def _():
        pl.semaphore_wait(known, 1)

    def norm_copy(j):
        return remote(norms.at[me], norms.at[me], send_c, recv_c, other(j))

    repeat(devices - 1, lambda j: norm_copy(j).start())

    def to_elem(j):
        to = me_e + (j + 1)
        to = jnp.where(to >= elems, to - elems, to)
        return remote(part_e.at[me_e], part_e.at[me_e], send_e, recv_e, dev(to, lead))

    def result(p):
        return remote(total_ref, total_ref, send_t.at[p], recv_t, dev(me_e, p))

    @pl.when(leading)
    def _():
        wait_bytes(part_p.at[pl.ds(0, params - 1)], recv_p)
        chip = part_p[0]
        for p in range(1, params):
            chip = chip + part_p[p]
        force = chip[:, wide:]
        force0 = force.astype(BF16)
        left = force - force0.astype(F32)
        force1 = left.astype(BF16)
        force2 = (left - force1.astype(F32)).astype(BF16)
        both = (((1,), (1,)), ((), ()))
        total = lax.dot_general(force2, ghost[...], both, preferred_element_type=F32)
        total = total + lax.dot_general(force1, ghost[...], both, preferred_element_type=F32)
        total = total + lax.dot_general(force0, ghost[...], both, preferred_element_type=F32)
        part_e[me_e] = chip[:, :wide]
        part_e[me_e, :, :modes] = chip[:, :modes] + total
        repeat(elems - 1, lambda j: to_elem(j).start())

    everyone = norms.at[pl.ds(0, devices - 1)]
    wait_bytes(everyone, recv_c)
    whole = norms[0]
    for d in range(1, devices):
        whole = whole + norms[d]
    diagonal = jnp.where(row == across, jnp.broadcast_to(whole, (snaps, 128)), 0.0)
    row_scale = jnp.sum(diagonal, axis=1, keepdims=True) / elem_total
    inverse = jnp.broadcast_to(1.0 / row_scale, (snaps, count))
    piece = cols_ref[...].reshape(modes, snaps, count) * inverse[None]
    training_ref[...] = piece.astype(BF16)

    every_elem = part_e.at[pl.ds(0, elems - 1)]

    @pl.when(leading)
    def _():
        wait_bytes(every_elem, recv_e)
        total = part_e[0]
        for e in range(1, elems):
            total = total + part_e[e]
        total_ref[...] = total
        for p in range(params - 1):
            result(p).start()

    @pl.when(jnp.logical_not(leading))
    def _():
        result(0).wait_recv()

    target_ref[...] = total_ref[:, :modes] / (row_scale * math.sqrt(elem_total))

    wait_bytes(others, send_n)
    wait_bytes(everyone, send_c)

    @pl.when(first)
    def _():
        to_relay().wait_send()

    @pl.when(jnp.logical_not(first))
    def _():
        wait_bytes(backs, send_d)

    @pl.when(relaying)
    def _():
        for q in range(params):
            wait_bytes(relay_disp, send_rd.at[q])
        ghost_from_relay().wait_send()

    @pl.when(leading)
    def _():
        ghost_copy().wait_send()
        for p in range(params - 1):
            hand_on(p).wait_send()
        wait_bytes(every_elem, send_e)
        for p in range(params - 1):
            result(p).wait_send()

    @pl.when(jnp.logical_not(leading))
    def _():
        to_lead().wait_send()


def finish_kernel(training_ref, target_ref, training_hbm, target_hbm, sem):
    copies = [
        pltpu.make_async_copy(target_ref, target_hbm, sem.at[0]),
        pltpu.make_async_copy(training_ref, training_hbm, sem.at[1]),
    ]
    for copy in copies:
        copy.start()
    for copy in copies:
        copy.wait()


def local(elems, params, coords, basis_rows, connectivity, modulus, stiffness):
    own_snaps, modes = coords.shape
    nodes = basis_rows.shape[2]
    count = connectivity.shape[0]
    snaps = own_snaps * params
    ghosts = nodes // 4
    if ghosts % 128 == 0:
        packed = (round_up(modes, 16), 3 * ghosts)
    else:
        packed = (round_up(modes, 16) + round_up(-(-modes // 2), 16), 2 * ghosts)
    edge = round_up(3 * ghosts + 32, 128)
    tiles = nodes // 128 + -(-ghosts // 128)
    wide = round_up(modes, 128)
    dofs = stiffness.shape[0]
    devices = elems * params
    inner = 4
    pairs = snaps // 2
    dma = pltpu.SemaphoreType.DMA
    vmem = pl.BlockSpec(memory_space=pltpu.VMEM)
    hbm = pl.BlockSpec(memory_space=pltpu.HBM)
    training, target = pl.pallas_call(
        functools.partial(kernel, elems, params, inner),
        out_shape=(
            jax.ShapeDtypeStruct((modes, snaps, count), BF16),
            jax.ShapeDtypeStruct((snaps, modes), F32),
        ),
        in_specs=[hbm] * 5,
        out_specs=(vmem, vmem),
        scratch_shapes=[
            pltpu.VMEM((own_snaps, modes), BF16),
            pltpu.VMEM((3, modes, nodes), BF16),
            pltpu.VMEM((8, count), jnp.int32),
            pltpu.VMEM((1, count), F32),
            pltpu.VMEM((dofs, dofs), F32),
            pltpu.VMEM(packed, BF16),
            pltpu.VMEM(packed, BF16),
            pltpu.VMEM((modes, edge), BF16),
            pltpu.VMEM((params, tiles, 3, own_snaps, 128), F32),
            pltpu.VMEM((pairs, dofs, 2 * count), F32),
            pltpu.VMEM((pairs if pairs <= 4 else 1, 3 * nodes, 2 * count), BF16),
            pltpu.VMEM((pairs, edge, 2 * count), BF16),
            pltpu.VMEM((pairs, modes, 2 * count), F32),
            pltpu.VMEM((modes * snaps, count), F32),
            pltpu.VMEM((wide, 128), F32),
            pltpu.VMEM((edge, 128), F32),
            pltpu.VMEM((devices, 1, 128), F32),
            pltpu.VMEM((params, snaps, wide + edge), F32),
            pltpu.VMEM((elems, snaps, wide), F32),
            pltpu.VMEM((snaps, wide), F32),
            pltpu.VMEM((params, tiles - nodes // 128, 3, own_snaps, 128), F32),
            pltpu.VMEM(packed, BF16),
            dma((4,)), dma, dma, dma, dma, dma, dma, dma, dma((params - 1,)), dma,
            dma, dma, dma, dma, dma, dma, dma((params - 1,)), dma,
            dma((params,)), dma, dma, dma,
            pltpu.SemaphoreType.REGULAR, pltpu.SemaphoreType.REGULAR,
        ],
        compiler_params=pltpu.CompilerParams(
            collective_id=0, has_side_effects=True, vmem_limit_bytes=40 * 1024 * 1024
        ),
    )(*(pltpu.with_memory_space_constraint(x, pltpu.HBM) for x in (
        coords, basis_rows, connectivity.T, modulus[None], stiffness
    )))
    training, target = pl.pallas_call(
        finish_kernel,
        out_shape=(
            jax.ShapeDtypeStruct((modes, snaps, count), BF16),
            jax.ShapeDtypeStruct((snaps, modes), F32),
        ),
        in_specs=[vmem, vmem],
        out_specs=(hbm, hbm),
        scratch_shapes=[dma((2,))],
        compiler_params=pltpu.CompilerParams(vmem_limit_bytes=20 * 1024 * 1024),
    )(training, target)
    return (jnp.transpose(training, (1, 0, 2)), target)


def solution(mesh):
    in_specs = (
        P("param", None),
        P(None, None, "elem"),
        P(("elem", "param"), None),
        P(("elem", "param")),
        P(),
    )
    out_specs = (P(None, None, ("elem", "param")), P())
    run = functools.partial(local, mesh.shape["elem"], mesh.shape["param"])
    return jax.shard_map(run, mesh=mesh, in_specs=in_specs, out_specs=out_specs, check_vma=False)
```

time: 22.4 us -> 19.9 us (0.89)
  Pallas kernels: 21.6 us -> 19.1 us
    pallas_call x1, Pallas kernels: 20.7 us -> 18.2 us  [local(): pl.pallas_call(functools.partial(kernel, elems, params, inner), out_shape...]
where the time goes in v3:
time: 19.9 us; the launch traced here: 19.7 us
  Pallas kernels  19.1 us (96%)
  between operations  0.64 us (3%)
    pallas_call x1, Pallas kernels, local(): pl.pallas_call(functools.partial(kernel, elems, params, inner), out_shape...  18.2 us
    pallas_call x1, Pallas kernels, local(): pl.pallas_call(finish_kernel, out_shape=(jax.ShapeDtypeStruct((modes, sna...  0.85 us

profile of v3, /device:TPU:0, one launch (start us, length us, event | category | flops | bytes accessed | tf_op | source)
XLA Modules:
  0.0 19.7 jit_solution(5709324813249782628)
XLA Ops:
  0.6 18.2 %shard_map.68 = (bf16[300,8,128]{2,1,0:T(8,128)(2,1)S(1)}, f32[8,300]{1,0:T(8,128)S(1)}) custom-call(bf16[4,300]{1,0:T(4,128)(2,1)} %coords_hbm.1, bf16[3,300,256]{2,1,0:T(8,128)(2,1)} %basis_hbm.1, s32[8,128]{1,0:T(8,128)} %bitcast.3, f32[1,128]{1,0:T(1,128)} %bitcast.4, f32[24,24]{1,0:T(8,128)} %stiff_hbm.1), custom_call_target="tpu_custom_call" | custom-call | tf_op jit(solution)/shard_map/pallas_call | solution.py:540
  18.9 0.8 %shard_map.69 = (bf16[300,8,128]{2,1,0:T(8,128)(2,1)}, f32[8,300]{1,0:T(8,128)}) custom-call(bf16[300,8,128]{2,1,0:T(8,128)(2,1)S(1)} %get-tuple-element.6.training_ref, f32[8,300]{1,0:T(8,128)S(1)} %get-tuple-element.7.target_ref), custom_call_target="tpu_custom_call" | custom-call | tf_op jit(solution)/shard_map/pallas_call | solution.py:582

commit v4 on v3

--- a/solution.py
+++ b/solution.py
@@ -29,9 +29,9 @@
 def kernel(
     elems, params, inner,
     coords_hbm, basis_hbm, conn_hbm, modulus_hbm, stiff_hbm,
-    training_ref, target_ref,
+    cols_ref, inverse_ref, target_ref,
     coords_ref, basis_ref, conn_ref, modulus_ref, stiff_ref,
-    packed, ghost_in, ghost, disp, corner_disp, weights, edge_weights, acc, cols_ref, part, nodal,
+    packed, ghost_in, ghost, disp, corner_disp, weights, edge_weights, acc, part, nodal,
     norms, part_p, part_e, total_ref, relay_disp, relay_ghost,
     load, load_b, send_g, recv_g, send_d, recv_d, send_n, recv_n, send_f, recv_f,
     send_c, recv_c, send_p, recv_p, send_e, recv_e, send_t, recv_t,
@@ -56,7 +56,7 @@
     leading = me_p == lead
     first, last = me_e == 0, me_e == elems - 1
     before = jnp.where(first, elems - 1, me_e - 1)
-    relay = elems // 4 * params + lead
+    relay = (elems // 4 + 1) * params + lead
     relaying = me == relay
     me_o, me_i = lax.div(me_e, inner), lax.rem(me_e, inner)
     bottom, top = me_o == 0, me_o == outer - 1
@@ -93,9 +93,6 @@
         copy.start()
 
     barrier = pltpu.get_barrier_semaphore()
-    below = jnp.logical_not(first) & (me_i == 0)
-    above = jnp.logical_not(last) & (me_i == inner - 1)
-
     @pl.when(first | last)
     def _():
         signal(barrier, relay)
@@ -106,12 +103,12 @@
             signal(barrier, dev(elems - 1, p))
             signal(barrier, dev(0, p))
 
-    @pl.when(below)
+    @pl.when(jnp.logical_not(first))
     def _():
         for p in range(params):
             signal(barrier, dev(me_e - 1, p))
 
-    @pl.when(above)
+    @pl.when(jnp.logical_not(last))
     def _():
         for p in range(params):
             signal(barrier, dev(me_e + 1, p))
@@ -124,15 +121,16 @@
     def _():
         signal(barrier, dev(me_e + inner, 0))
 
-    plane = inner * params
-    place = me_i * params + me_p
-    for j in range(1, plane):
-        to = place + j
-        signal(barrier, me_o * plane + jnp.where(to >= plane, to - plane, to))
-    greeted = plane - 1 + jnp.where(first | last, 1, 0) + jnp.where(relaying, 2 * params, 0)
-    greeted += jnp.where(below, params, 0) + jnp.where(above, params, 0)
-    greeted += jnp.where(climbing & jnp.logical_not(bottom), 1, 0)
-    greeted += jnp.where(climbing & jnp.logical_not(top), 1, 0)
+    for j in range(1, params):
+        to = me_p + j
+        signal(barrier, dev(me_e, jnp.where(to >= params, to - params, to)))
+    for j in range(1, inner):
+        to = me_i + j
+        signal(barrier, dev(me_o * inner + jnp.where(to >= inner, to - inner, to), 0))
+    greeted = params - 1 + jnp.where(first | last, 1, params) + params
+    greeted += jnp.where(relaying, 2 * params, 0)
+    climbs = (inner - 1) * params + 2 - jnp.where(bottom | top, 1, 0)
+    greeted += jnp.where(climbing, climbs, 0)
 
     part[...] = jnp.zeros_like(part)
     nodal[...] = jnp.zeros_like(nodal)
@@ -424,6 +422,8 @@
         to = jnp.where(to >= elems, to - elems, to)
         return remote(part_e.at[me_e], part_e.at[me_e], send_e, recv_e, dev(to, lead))
 
+    every_elem = part_e.at[pl.ds(0, elems - 1)]
+
     def result(p):
         return remote(total_ref, total_ref, send_t.at[p], recv_t, dev(me_e, p))
 
@@ -445,6 +445,13 @@
         part_e[me_e] = chip[:, :wide]
         part_e[me_e, :, :modes] = chip[:, :modes] + total
         repeat(elems - 1, lambda j: to_elem(j).start())
+        wait_bytes(every_elem, recv_e)
+        total = part_e[0]
+        for e in range(1, elems):
+            total = total + part_e[e]
+        total_ref[...] = total
+        for p in range(params - 1):
+            result(p).start()
 
     everyone = norms.at[pl.ds(0, devices - 1)]
     wait_bytes(everyone, recv_c)
@@ -453,21 +460,7 @@
         whole = whole + norms[d]
     diagonal = jnp.where(row == across, jnp.broadcast_to(whole, (snaps, 128)), 0.0)
     row_scale = jnp.sum(diagonal, axis=1, keepdims=True) / elem_total
-    inverse = jnp.broadcast_to(1.0 / row_scale, (snaps, count))
-    piece = cols_ref[...].reshape(modes, snaps, count) * inverse[None]
-    training_ref[...] = piece.astype(BF16)
-
-    every_elem = part_e.at[pl.ds(0, elems - 1)]
-
-    @pl.when(leading)
-    def _():
-        wait_bytes(every_elem, recv_e)
-        total = part_e[0]
-        for e in range(1, elems):
-            total = total + part_e[e]
-        total_ref[...] = total
-        for p in range(params - 1):
-            result(p).start()
+    inverse_ref[...] = jnp.broadcast_to(1.0 / row_scale, (snaps, count))
 
     @pl.when(jnp.logical_not(leading))
     def _():
@@ -506,13 +499,19 @@
         to_lead().wait_send()
 
 
-def finish_kernel(training_ref, target_ref, training_hbm, target_hbm, sem):
-    copies = [
-        pltpu.make_async_copy(target_ref, target_hbm, sem.at[0]),
-        pltpu.make_async_copy(training_ref, training_hbm, sem.at[1]),
-    ]
-    for copy in copies:
-        copy.start()
+def finish_kernel(cols_ref, inverse_ref, target_ref, training_hbm, target_hbm, training, sem):
+    modes, snaps, count = training.shape
+    copies = [pltpu.make_async_copy(target_ref, target_hbm, sem.at[0])]
+    copies[0].start()
+    inverse = inverse_ref[...][None]
+    chunks = sem.shape[0] - 1
+    size = modes // chunks
+    for c in range(chunks):
+        rows = pl.ds(c * size, size)
+        piece = cols_ref[c * size * snaps : (c + 1) * size * snaps]
+        training[rows] = (piece.reshape(size, snaps, count) * inverse).astype(BF16)
+        copies.append(pltpu.make_async_copy(training.at[rows], training_hbm.at[rows], sem.at[c + 1]))
+        copies[-1].start()
     for copy in copies:
         copy.wait()
 
@@ -537,14 +536,15 @@
     dma = pltpu.SemaphoreType.DMA
     vmem = pl.BlockSpec(memory_space=pltpu.VMEM)
     hbm = pl.BlockSpec(memory_space=pltpu.HBM)
-    training, target = pl.pallas_call(
+    cols, inverse, target = pl.pallas_call(
         functools.partial(kernel, elems, params, inner),
         out_shape=(
-            jax.ShapeDtypeStruct((modes, snaps, count), BF16),
+            jax.ShapeDtypeStruct((modes * snaps, count), F32),
+            jax.ShapeDtypeStruct((snaps, count), F32),
             jax.ShapeDtypeStruct((snaps, modes), F32),
         ),
         in_specs=[hbm] * 5,
-        out_specs=(vmem, vmem),
+        out_specs=(vmem, vmem, vmem),
         scratch_shapes=[
             pltpu.VMEM((own_snaps, modes), BF16),
             pltpu.VMEM((3, modes, nodes), BF16),
@@ -559,7 +559,6 @@
             pltpu.VMEM((pairs if pairs <= 4 else 1, 3 * nodes, 2 * count), BF16),
             pltpu.VMEM((pairs, edge, 2 * count), BF16),
             pltpu.VMEM((pairs, modes, 2 * count), F32),
-            pltpu.VMEM((modes * snaps, count), F32),
             pltpu.VMEM((wide, 128), F32),
             pltpu.VMEM((edge, 128), F32),
             pltpu.VMEM((devices, 1, 128), F32),
@@ -579,17 +578,18 @@
     )(*(pltpu.with_memory_space_constraint(x, pltpu.HBM) for x in (
         coords, basis_rows, connectivity.T, modulus[None], stiffness
     )))
+    chunks = next(c for c in (4, 3, 2, 1) if modes % c == 0)
     training, target = pl.pallas_call(
         finish_kernel,
         out_shape=(
             jax.ShapeDtypeStruct((modes, snaps, count), BF16),
             jax.ShapeDtypeStruct((snaps, modes), F32),
         ),
-        in_specs=[vmem, vmem],
+        in_specs=[vmem, vmem, vmem],
         out_specs=(hbm, hbm),
-        scratch_shapes=[dma((2,))],
+        scratch_shapes=[pltpu.VMEM((modes, snaps, count), BF16), dma((chunks + 1,))],
         compiler_params=pltpu.CompilerParams(vmem_limit_bytes=20 * 1024 * 1024),
-    )(training, target)
+    )(cols, inverse, target)
     return (jnp.transpose(training, (1, 0, 2)), target)
 
 

time: 19.9 us -> 19 us (0.955)
  Pallas kernels: 19.1 us -> 18.2 us
    pallas_call x1, Pallas kernels: 18.2 us -> 17.3 us  [local(): pl.pallas_call(functools.partial(kernel, elems, params, inner), out_shape...]
where the time goes in v4:
time: 19 us; the launch traced here: 18.8 us
  Pallas kernels  18.2 us (96%)
  between operations  0.64 us (3%)
    pallas_call x1, Pallas kernels, local(): pl.pallas_call(functools.partial(kernel, elems, params, inner), out_shape...  17.3 us
    pallas_call x1, Pallas kernels, local(): pl.pallas_call(finish_kernel, out_shape=(jax.ShapeDtypeStruct((modes, sna...  0.88 us

profile of v4, /device:TPU:0, one launch (start us, length us, event | category | flops | bytes accessed | tf_op | source)
XLA Modules:
  0.0 18.8 jit_solution(10825802191188320552)
XLA Ops:
  0.6 17.3 %shard_map.68 = (f32[2400,128]{1,0:T(8,128)S(1)}, f32[8,128]{1,0:T(8,128)S(1)}, f32[8,300]{1,0:T(8,128)S(1)}) custom-call(bf16[4,300]{1,0:T(4,128)(2,1)} %coords_hbm.1, bf16[3,300,256]{2,1,0:T(8,128)(2,1)} %basis_hbm.1, s32[8,128]{1,0:T(8,128)} %bitcast.3, f32[1,128]{1,0:T(1,128)} %bitcast.4, f32[24,24]{1,0:T(8,128)} %stiff_hbm.1), custom_call_target="tpu_custom_call" | custom-call | tf_op jit(solution)/shard_map/pallas_call | solution.py:539
  17.9 0.9 %shard_map.69 = (bf16[300,8,128]{2,1,0:T(8,128)(2,1)}, f32[8,300]{1,0:T(8,128)}) custom-call(f32[2400,128]{1,0:T(8,128)S(1)} %get-tuple-element.7.cols_ref, f32[8,128]{1,0:T(8,128)S(1)} %get-tuple-element.8.inverse_ref, f32[8,300]{1,0:T(8,128)S(1)} %get-tuple-element.9.target_ref), custom_call_target="tpu_custom_call" | custom-call | tf_op jit(solution)/shard_map/pallas_call | solution.py:582

commit v5 on v4

--- a/solution.py
+++ b/solution.py
@@ -12,6 +12,7 @@
 F32 = jnp.float32
 BF16 = jnp.bfloat16
 UNROLL = 64
+CHUNKS = 4
 
 
 def round_up(value, to):
@@ -33,10 +34,12 @@
     coords_ref, basis_ref, conn_ref, modulus_ref, stiff_ref,
     packed, ghost_in, ghost, disp, corner_disp, weights, edge_weights, acc, part, nodal,
     norms, part_p, part_e, total_ref, relay_disp, relay_ghost,
-    load, load_b, send_g, recv_g, send_d, recv_d, send_n, recv_n, send_f, recv_f,
-    send_c, recv_c, send_p, recv_p, send_e, recv_e, send_t, recv_t,
+    load, load_b, send_g, recv_g, recv_d, recv_n, send_f, recv_f,
+    recv_c, recv_p, recv_e, send_t, recv_t,
     send_rd, recv_rd, send_rg, recv_rg, climb, known,
 ):
+    send_d, send_n, send_p, send_e = [load.at[i] for i in range(4)]
+    send_c = load_b
     own_snaps, modes = coords_hbm.shape
     dofs = stiff_hbm.shape[0]
     snaps = own_snaps * params
@@ -60,7 +63,8 @@
     relaying = me == relay
     me_o, me_i = lax.div(me_e, inner), lax.rem(me_e, inner)
     bottom, top = me_o == 0, me_o == outer - 1
-    climbing = me_p == 0
+    guide = inner // 2
+    climbing = (me_p == 0) & (me_i == guide)
 
     def dev(e, p):
         return e * params + p
@@ -124,9 +128,11 @@
     for j in range(1, params):
         to = me_p + j
         signal(barrier, dev(me_e, jnp.where(to >= params, to - params, to)))
-    for j in range(1, inner):
-        to = me_i + j
-        signal(barrier, dev(me_o * inner + jnp.where(to >= inner, to - inner, to), 0))
+
+    @pl.when(me_i != guide)
+    def _():
+        signal(barrier, dev(me_o * inner + guide, 0))
+
     greeted = params - 1 + jnp.where(first | last, 1, params) + params
     greeted += jnp.where(relaying, 2 * params, 0)
     climbs = (inner - 1) * params + 2 - jnp.where(bottom | top, 1, 0)
@@ -179,17 +185,24 @@
             relay_disp.at[q], disp.at[q, ghost_part], send_rd.at[q], recv_d, dev(elems - 1, p)
         )
 
-    def ghost_copy():
-        return remote(packed, ghost_in, send_g, recv_g, dev(before, lead))
-
-    def ghost_to_relay():
-        return remote(packed, relay_ghost, send_g, recv_rg, relay)
-
-    def ghost_from_relay():
-        return remote(relay_ghost, ghost_in, send_rg, recv_g, dev(elems - 1, lead))
-
-    def hand_on(p):
-        return remote(ghost_in, ghost_in, send_f.at[p], recv_f, dev(me_e, p))
+    cuts = [rows // 16 * c // CHUNKS * 16 for c in range(CHUNKS + 1)]
+
+    def cut(ref, c):
+        return ref.at[pl.ds(cuts[c], cuts[c + 1] - cuts[c])]
+
+    def ghost_copy(c):
+        return remote(cut(packed, c), cut(ghost_in, c), send_g, recv_g.at[c], dev(before, lead))
+
+    def ghost_to_relay(c):
+        return remote(cut(packed, c), cut(relay_ghost, c), send_g, recv_rg.at[c], relay)
+
+    def ghost_from_relay(c):
+        return remote(
+            cut(relay_ghost, c), cut(ghost_in, c), send_rg, recv_g.at[c], dev(elems - 1, lead)
+        )
+
+    def hand_on(p, c):
+        return remote(cut(ghost_in, c), cut(ghost_in, c), send_f.at[p], recv_f, dev(me_e, p))
 
     @pl.when(first)
     def _():
@@ -202,11 +215,13 @@
 
     @pl.when(first & leading)
     def _():
-        ghost_to_relay().start()
+        for c in range(CHUNKS):
+            ghost_to_relay(c).start()
 
     @pl.when(jnp.logical_not(first) & leading)
     def _():
-        ghost_copy().start()
+        for c in range(CHUNKS):
+            ghost_copy(c).start()
 
     for p in range(1, params):
         own_disp(p).start()
@@ -216,9 +231,10 @@
         wait_bytes(relay_disp, recv_rd)
         for q in range(params):
             for p in range(params):
-                from_relay(q, params - 1 - p).start()
-        ghost_to_relay().wait_recv()
-        ghost_from_relay().start()
+                from_relay(q, p).start()
+        for c in range(CHUNKS):
+            ghost_to_relay(c).wait_recv()
+            ghost_from_relay(c).start()
 
     @pl.when(climbing & jnp.logical_not(bottom))
     def _():
@@ -230,11 +246,7 @@
 
     @pl.when(climbing & top)
     def _():
-        for p in range(1, params):
-            signal(known, dev(me_e, p))
-        for o in range(outer - 1):
-            for p in range(params):
-                signal(known, dev(o * inner + me_i, p))
+        repeat(devices - 1, lambda j: signal(known, other(j)))
 
     corners = conn_ref[...]
     base = jnp.min(corners, axis=0, keepdims=True)
@@ -370,6 +382,14 @@
 
     part_p[me_p, :, :wide] = flipped(part)
     wait_bytes(backs, recv_d)
+
+    @pl.when(leading)
+    def _():
+        for c in range(CHUNKS):
+            ghost_copy(c).wait_recv()
+            for p in range(params - 1):
+                hand_on(p, c).start()
+
     each_pair(edge_forces)
     part_p[me_p, :, wide:] = flipped(nodal)
 
@@ -380,15 +400,9 @@
     def _():
         to_lead().start()
 
-    @pl.when(leading)
-    def _():
-        ghost_copy().wait_recv()
-        for p in range(params - 1):
-            hand_on(p).start()
-
     @pl.when(jnp.logical_not(leading))
     def _():
-        hand_on(0).wait_recv()
+        wait_bytes(ghost_in, recv_f)
 
     if ghosts % 128 == 0:
         ghost[:, :tail_at] = ghost_in[:modes]
@@ -396,6 +410,16 @@
         ghost[:, : 2 * ghosts] = ghost_in[:modes]
         ghost[:half, 2 * ghosts : tail_at] = ghost_in[rows - half :, :ghosts]
         ghost[half:, 2 * ghosts : tail_at] = ghost_in[rows - half : rows - 2 * half + modes, ghosts:]
+    def to_elem(j):
+        to = me_e + (j + 1)
+        to = jnp.where(to >= elems, to - elems, to)
+        return remote(part_e.at[me_e], part_e.at[me_e], send_e, recv_e, dev(to, lead))
+
+    every_elem = part_e.at[pl.ds(0, elems - 1)]
+
+    def result(p):
+        return remote(total_ref, total_ref, send_t.at[p], recv_t, dev(me_e, p))
+
     row = lax.broadcasted_iota(jnp.int32, (snaps, 128), 0)
     across = lax.broadcasted_iota(jnp.int32, (snaps, 128), 1)
     squares = jnp.zeros((snaps, count), F32)
@@ -416,16 +440,6 @@
         return remote(norms.at[me], norms.at[me], send_c, recv_c, other(j))
 
     repeat(devices - 1, lambda j: norm_copy(j).start())
-
-    def to_elem(j):
-        to = me_e + (j + 1)
-        to = jnp.where(to >= elems, to - elems, to)
-        return remote(part_e.at[me_e], part_e.at[me_e], send_e, recv_e, dev(to, lead))
-
-    every_elem = part_e.at[pl.ds(0, elems - 1)]
-
-    def result(p):
-        return remote(total_ref, total_ref, send_t.at[p], recv_t, dev(me_e, p))
 
     @pl.when(leading)
     def _():
@@ -483,13 +497,13 @@
     def _():
         for q in range(params):
             wait_bytes(relay_disp, send_rd.at[q])
-        ghost_from_relay().wait_send()
+        wait_bytes(relay_ghost, send_rg)
 
     @pl.when(leading)
     def _():
-        ghost_copy().wait_send()
+        wait_bytes(packed, send_g)
         for p in range(params - 1):
-            hand_on(p).wait_send()
+            wait_bytes(ghost_in, send_f.at[p])
         wait_bytes(every_elem, send_e)
         for p in range(params - 1):
             result(p).wait_send()
@@ -567,9 +581,9 @@
             pltpu.VMEM((snaps, wide), F32),
             pltpu.VMEM((params, tiles - nodes // 128, 3, own_snaps, 128), F32),
             pltpu.VMEM(packed, BF16),
-            dma((4,)), dma, dma, dma, dma, dma, dma, dma, dma((params - 1,)), dma,
-            dma, dma, dma, dma, dma, dma, dma((params - 1,)), dma,
-            dma((params,)), dma, dma, dma,
+            dma((4,)), dma, dma, dma((CHUNKS,)), dma, dma, dma((params - 1,)), dma,
+            dma, dma, dma, dma((params - 1,)), dma,
+            dma((params,)), dma, dma, dma((CHUNKS,)),
             pltpu.SemaphoreType.REGULAR, pltpu.SemaphoreType.REGULAR,
         ],
         compiler_params=pltpu.CompilerParams(

time: 19 us -> 18.6 us (0.979)
  Pallas kernels: 18.2 us -> 17.8 us
    pallas_call x1, Pallas kernels: 17.3 us -> 16.9 us  [local(): pl.pallas_call(functools.partial(kernel, elems, params, inner), out_shape...]
where the time goes in v5:
time: 18.6 us; the launch traced here: 18.4 us
  Pallas kernels  17.8 us (96%)
  between operations  0.64 us (3%)
    pallas_call x1, Pallas kernels, local(): pl.pallas_call(functools.partial(kernel, elems, params, inner), out_shape...  16.9 us
    pallas_call x1, Pallas kernels, local(): pl.pallas_call(finish_kernel, out_shape=(jax.ShapeDtypeStruct((modes, sna...  0.88 us

profile of v5, /device:TPU:0, one launch (start us, length us, event | category | flops | bytes accessed | tf_op | source)
XLA Modules:
  0.0 18.4 jit_solution(1256103785724393789)
XLA Ops:
  0.6 16.9 %shard_map.68 = (f32[2400,128]{1,0:T(8,128)S(1)}, f32[8,128]{1,0:T(8,128)S(1)}, f32[8,300]{1,0:T(8,128)S(1)}) custom-call(bf16[4,300]{1,0:T(4,128)(2,1)} %coords_hbm.1, bf16[3,300,256]{2,1,0:T(8,128)(2,1)} %basis_hbm.1, s32[8,128]{1,0:T(8,128)} %bitcast.3, f32[1,128]{1,0:T(1,128)} %bitcast.4, f32[24,24]{1,0:T(8,128)} %stiff_hbm.1), custom_call_target="tpu_custom_call" | custom-call | tf_op jit(solution)/shard_map/pallas_call | solution.py:553
  17.5 0.9 %shard_map.69 = (bf16[300,8,128]{2,1,0:T(8,128)(2,1)}, f32[8,300]{1,0:T(8,128)}) custom-call(f32[2400,128]{1,0:T(8,128)S(1)} %get-tuple-element.7.cols_ref, f32[8,128]{1,0:T(8,128)S(1)} %get-tuple-element.8.inverse_ref, f32[8,300]{1,0:T(8,128)S(1)} %get-tuple-element.9.target_ref), custom_call_target="tpu_custom_call" | custom-call | tf_op jit(solution)/shard_map/pallas_call | solution.py:596

commit v6 on v5

--- a/solution.py
+++ b/solution.py
@@ -59,7 +59,7 @@
     leading = me_p == lead
     first, last = me_e == 0, me_e == elems - 1
     before = jnp.where(first, elems - 1, me_e - 1)
-    relay = (elems // 4 + 1) * params + lead
+    relay = (elems // 4 + 2) * params + lead
     relaying = me == relay
     me_o, me_i = lax.div(me_e, inner), lax.rem(me_e, inner)
     bottom, top = me_o == 0, me_o == outer - 1
@@ -180,10 +180,8 @@
     def to_relay():
         return remote(front, relay_disp.at[me_p], send_d, recv_rd, relay)
 
-    def from_relay(q, p):
-        return remote(
-            relay_disp.at[q], disp.at[q, ghost_part], send_rd.at[q], recv_d, dev(elems - 1, p)
-        )
+    def from_relay(p):
+        return remote(relay_disp, backs, send_rd.at[p], recv_d, dev(elems - 1, p))
 
     cuts = [rows // 16 * c // CHUNKS * 16 for c in range(CHUNKS + 1)]
 
@@ -218,7 +216,7 @@
         for c in range(CHUNKS):
             ghost_to_relay(c).start()
 
-    @pl.when(jnp.logical_not(first) & leading)
+    @pl.when(jnp.logical_not(first | relaying) & leading)
     def _():
         for c in range(CHUNKS):
             ghost_copy(c).start()
@@ -229,12 +227,13 @@
     @pl.when(relaying)
     def _():
         wait_bytes(relay_disp, recv_rd)
-        for q in range(params):
-            for p in range(params):
-                from_relay(q, p).start()
+        for p in range(params):
+            from_relay(p).start()
         for c in range(CHUNKS):
             ghost_to_relay(c).wait_recv()
             ghost_from_relay(c).start()
+        for c in range(CHUNKS):
+            ghost_copy(c).start()
 
     @pl.when(climbing & jnp.logical_not(bottom))
     def _():
@@ -422,42 +421,50 @@
 
     row = lax.broadcasted_iota(jnp.int32, (snaps, 128), 0)
     across = lax.broadcasted_iota(jnp.int32, (snaps, 128), 1)
-    squares = jnp.zeros((snaps, count), F32)
-    if pairs <= 4:
-        for p in range(pairs):
-            squares = whole_product(p, squares)
-    else:
-        squares = lax.fori_loop(0, pairs, whole_product, squares)
-
-    norm = jnp.sum(jnp.sqrt(squares), axis=1, keepdims=True)
-    norms[me] = jnp.sum(jnp.where(row == across, norm, 0.0), axis=0, keepdims=True)
-
-    @pl.when(jnp.logical_not(climbing & top))
-    def _():
-        pl.semaphore_wait(known, 1)
-
-    def norm_copy(j):
-        return remote(norms.at[me], norms.at[me], send_c, recv_c, other(j))
-
-    repeat(devices - 1, lambda j: norm_copy(j).start())
+
+    def finish_norm():
+        squares = jnp.zeros((snaps, count), F32)
+        if pairs <= 4:
+            for p in range(pairs):
+                squares = whole_product(p, squares)
+        else:
+            squares = lax.fori_loop(0, pairs, whole_product, squares)
+        norm = jnp.sum(jnp.sqrt(squares), axis=1, keepdims=True)
+        norms[me] = jnp.sum(jnp.where(row == across, norm, 0.0), axis=0, keepdims=True)
+
+    @pl.when(jnp.logical_not(leading))
+    def _():
+        finish_norm()
 
     @pl.when(leading)
     def _():
         wait_bytes(part_p.at[pl.ds(0, params - 1)], recv_p)
+        finish_norm()
         chip = part_p[0]
         for p in range(1, params):
             chip = chip + part_p[p]
         force = chip[:, wide:]
-        force0 = force.astype(BF16)
-        left = force - force0.astype(F32)
-        force1 = left.astype(BF16)
-        force2 = (left - force1.astype(F32)).astype(BF16)
+        high = force.astype(BF16).astype(F32)
+        left = force - high
+        mid = left.astype(BF16).astype(F32)
+        forces = jnp.concatenate([left - mid, mid, high], axis=0).astype(BF16)
         both = (((1,), (1,)), ((), ()))
-        total = lax.dot_general(force2, ghost[...], both, preferred_element_type=F32)
-        total = total + lax.dot_general(force1, ghost[...], both, preferred_element_type=F32)
-        total = total + lax.dot_general(force0, ghost[...], both, preferred_element_type=F32)
+        parts = lax.dot_general(forces, ghost[...], both, preferred_element_type=F32)
+        total = parts[:snaps] + parts[snaps : 2 * snaps] + parts[2 * snaps :]
         part_e[me_e] = chip[:, :wide]
         part_e[me_e, :, :modes] = chip[:, :modes] + total
+
+    @pl.when(jnp.logical_not(climbing & top))
+    def _():
+        pl.semaphore_wait(known, 1)
+
+    def norm_copy(j):
+        return remote(norms.at[me], norms.at[me], send_c, recv_c, other(j))
+
+    repeat(devices - 1, lambda j: norm_copy(j).start())
+
+    @pl.when(leading)
+    def _():
         repeat(elems - 1, lambda j: to_elem(j).start())
         wait_bytes(every_elem, recv_e)
         total = part_e[0]
@@ -495,8 +502,8 @@
 
     @pl.when(relaying)
     def _():
-        for q in range(params):
-            wait_bytes(relay_disp, send_rd.at[q])
+        for p in range(params):
+            wait_bytes(relay_disp, send_rd.at[p])
         wait_bytes(relay_ghost, send_rg)
 
     @pl.when(leading)

time: 18.6 us -> 18.3 us (0.984)
  Pallas kernels: 17.8 us -> 17.5 us
    pallas_call x1, Pallas kernels: 16.9 us -> 16.6 us  [local(): pl.pallas_call(functools.partial(kernel, elems, params, inner), out_shape...]
where the time goes in v6:
time: 18.3 us; the launch traced here: 18.1 us
  Pallas kernels  17.5 us (96%)
  between operations  0.64 us (3%)
    pallas_call x1, Pallas kernels, local(): pl.pallas_call(functools.partial(kernel, elems, params, inner), out_shape...  16.6 us
    pallas_call x1, Pallas kernels, local(): pl.pallas_call(finish_kernel, out_shape=(jax.ShapeDtypeStruct((modes, sna...  0.88 us

profile of v6, /device:TPU:0, one launch (start us, length us, event | category | flops | bytes accessed | tf_op | source)
XLA Modules:
  0.0 18.1 jit_solution(10868715461526491386)
XLA Ops:
  0.6 16.6 %shard_map.68 = (f32[2400,128]{1,0:T(8,128)S(1)}, f32[8,128]{1,0:T(8,128)S(1)}, f32[8,300]{1,0:T(8,128)S(1)}) custom-call(bf16[4,300]{1,0:T(4,128)(2,1)} %coords_hbm.1, bf16[3,300,256]{2,1,0:T(8,128)(2,1)} %basis_hbm.1, s32[8,128]{1,0:T(8,128)} %bitcast.3, f32[1,128]{1,0:T(1,128)} %bitcast.4, f32[24,24]{1,0:T(8,128)} %stiff_hbm.1), custom_call_target="tpu_custom_call" | custom-call | tf_op jit(solution)/shard_map/pallas_call | solution.py:560
  17.2 0.9 %shard_map.69 = (bf16[300,8,128]{2,1,0:T(8,128)(2,1)}, f32[8,300]{1,0:T(8,128)}) custom-call(f32[2400,128]{1,0:T(8,128)S(1)} %get-tuple-element.7.cols_ref, f32[8,128]{1,0:T(8,128)S(1)} %get-tuple-element.8.inverse_ref, f32[8,300]{1,0:T(8,128)S(1)} %get-tuple-element.9.target_ref), custom_call_target="tpu_custom_call" | custom-call | tf_op jit(solution)/shard_map/pallas_call | solution.py:603

commit v7 on v6

--- a/solution.py
+++ b/solution.py
@@ -12,7 +12,8 @@
 F32 = jnp.float32
 BF16 = jnp.bfloat16
 UNROLL = 64
-CHUNKS = 4
+CHUNKS = 5
+FAR = 2
 
 
 def round_up(value, to):
@@ -152,16 +153,14 @@
         moved = moved.astype(BF16).astype(F32)
         for t in range(own_tiles):
             disp[me_p, t, k] = moved[:, t * 128 : (t + 1) * 128]
-    rows = packed.shape[0]
-    if ghosts % 128 == 0:
-        for k in range(3):
-            packed[:modes, k * ghosts : (k + 1) * ghosts] = basis_ref[k, :, :ghosts]
-    else:
-        half = rows - round_up(modes, 16)
-        packed[:modes, :ghosts] = basis_ref[0, :, :ghosts]
-        packed[:modes, ghosts:] = basis_ref[1, :, :ghosts]
-        packed[rows - half :, :ghosts] = basis_ref[2, :half, :ghosts]
-        packed[rows - half : rows - 2 * half + modes, ghosts:] = basis_ref[2, half:, :ghosts]
+    rows, lanes = packed.shape
+    a_rows = round_up(modes, 16)
+    half = rows - a_rows
+    if half:
+        packed[:half, :ghosts] = basis_ref[2, :half, :ghosts]
+        packed[: modes - half, ghosts:] = basis_ref[2, half:, :ghosts]
+    for k in range(lanes // ghosts):
+        packed[half : half + modes, k * ghosts : (k + 1) * ghosts] = basis_ref[k, :, :ghosts]
 
     pl.semaphore_wait(barrier, greeted)
     own_part, ghost_part = pl.ds(0, own_tiles), pl.ds(own_tiles, ghost_tiles)
@@ -183,7 +182,10 @@
     def from_relay(p):
         return remote(relay_disp, backs, send_rd.at[p], recv_d, dev(elems - 1, p))
 
-    cuts = [rows // 16 * c // CHUNKS * 16 for c in range(CHUNKS + 1)]
+    fore = 2 if half else 0
+    rear = CHUNKS - fore
+    cuts = [half // 16 * c // fore * 16 for c in range(fore)]
+    cuts += [half + a_rows // 16 * c // rear * 16 for c in range(rear + 1)]
 
     def cut(ref, c):
         return ref.at[pl.ds(cuts[c], cuts[c + 1] - cuts[c])]
@@ -200,7 +202,11 @@
         )
 
     def hand_on(p, c):
-        return remote(cut(ghost_in, c), cut(ghost_in, c), send_f.at[p], recv_f, dev(me_e, p))
+        to = cut(ghost_in, c)
+        if c >= fore:
+            to = ghost.at[pl.ds(cuts[c] - half, cuts[c + 1] - cuts[c]), pl.ds(0, lanes)]
+        kind = 0 if c < fore else 1
+        return remote(cut(ghost_in, c), to, send_f.at[p], recv_f.at[kind], dev(me_e, p))
 
     @pl.when(first)
     def _():
@@ -275,7 +281,7 @@
     start = tail_at // 128 * 128
     blank = [jnp.zeros((modes, tail_at - start), BF16)] if tail_at > start else []
     after = [jnp.zeros((modes, edge - tail_at - 24), BF16)]
-    ghost[:, start:] = jnp.concatenate(blank + tails + after, axis=1)
+    ghost[:modes, start:] = jnp.concatenate(blank + tails + after, axis=1)
 
     def gathered(p, found, tiles):
         pieces = []
@@ -352,7 +358,7 @@
             nodal[at_rows] = jnp.where(lane == 2 * p + at, total, nodal[at_rows])
 
     def whole_product(p, squares):
-        result = acc[p] + jnp.dot(ghost[...], edge_weights[p], preferred_element_type=F32)
+        result = acc[p] + jnp.dot(ghost[:modes], edge_weights[p], preferred_element_type=F32)
         for at in range(2):
             s = 2 * p + at
             mine = result[:, at * count : (at + 1) * count]
@@ -399,16 +405,11 @@
     def _():
         to_lead().start()
 
-    @pl.when(jnp.logical_not(leading))
-    def _():
-        wait_bytes(ghost_in, recv_f)
-
-    if ghosts % 128 == 0:
-        ghost[:, :tail_at] = ghost_in[:modes]
-    else:
-        ghost[:, : 2 * ghosts] = ghost_in[:modes]
-        ghost[:half, 2 * ghosts : tail_at] = ghost_in[rows - half :, :ghosts]
-        ghost[half:, 2 * ghosts : tail_at] = ghost_in[rows - half : rows - 2 * half + modes, ghosts:]
+    def unfold():
+        if half:
+            ghost[:half, lanes:tail_at] = ghost_in[:half, :ghosts]
+            ghost[half:modes, lanes:tail_at] = ghost_in[: modes - half, ghosts:]
+
     def to_elem(j):
         to = me_e + (j + 1)
         to = jnp.where(to >= elems, to - elems, to)
@@ -434,10 +435,16 @@
 
     @pl.when(jnp.logical_not(leading))
     def _():
+        if half:
+            wait_bytes(ghost_in.at[pl.ds(0, half)], recv_f.at[0])
+        unfold()
+        wait_bytes(ghost.at[:, pl.ds(0, lanes)], recv_f.at[1])
         finish_norm()
 
     @pl.when(leading)
     def _():
+        ghost[:modes, :lanes] = ghost_in[half : half + modes]
+        unfold()
         wait_bytes(part_p.at[pl.ds(0, params - 1)], recv_p)
         finish_norm()
         chip = part_p[0]
@@ -449,7 +456,7 @@
         mid = left.astype(BF16).astype(F32)
         forces = jnp.concatenate([left - mid, mid, high], axis=0).astype(BF16)
         both = (((1,), (1,)), ((), ()))
-        parts = lax.dot_general(forces, ghost[...], both, preferred_element_type=F32)
+        parts = lax.dot_general(forces, ghost[:modes], both, preferred_element_type=F32)
         total = parts[:snaps] + parts[snaps : 2 * snaps] + parts[2 * snaps :]
         part_e[me_e] = chip[:, :wide]
         part_e[me_e, :, :modes] = chip[:, :modes] + total
@@ -461,11 +468,16 @@
     def norm_copy(j):
         return remote(norms.at[me], norms.at[me], send_c, recv_c, other(j))
 
+    @pl.when(leading)
+    def _():
+        for j in range(FAR):
+            to_elem(j).start()
+
     repeat(devices - 1, lambda j: norm_copy(j).start())
 
     @pl.when(leading)
     def _():
-        repeat(elems - 1, lambda j: to_elem(j).start())
+        repeat(elems - 1 - FAR, lambda j: to_elem(j + FAR).start())
         wait_bytes(every_elem, recv_e)
         total = part_e[0]
         for e in range(1, elems):
@@ -574,7 +586,7 @@
             pltpu.VMEM((dofs, dofs), F32),
             pltpu.VMEM(packed, BF16),
             pltpu.VMEM(packed, BF16),
-            pltpu.VMEM((modes, edge), BF16),
+            pltpu.VMEM((round_up(modes, 16), edge), BF16),
             pltpu.VMEM((params, tiles, 3, own_snaps, 128), F32),
             pltpu.VMEM((pairs, dofs, 2 * count), F32),
             pltpu.VMEM((pairs if pairs <= 4 else 1, 3 * nodes, 2 * count), BF16),
@@ -588,7 +600,7 @@
             pltpu.VMEM((snaps, wide), F32),
             pltpu.VMEM((params, tiles - nodes // 128, 3, own_snaps, 128), F32),
             pltpu.VMEM(packed, BF16),
-            dma((4,)), dma, dma, dma((CHUNKS,)), dma, dma, dma((params - 1,)), dma,
+            dma((4,)), dma, dma, dma((CHUNKS,)), dma, dma, dma((params - 1,)), dma((2,)),
             dma, dma, dma, dma((params - 1,)), dma,
             dma((params,)), dma, dma, dma((CHUNKS,)),
             pltpu.SemaphoreType.REGULAR, pltpu.SemaphoreType.REGULAR,

time: 18.3 us -> 18.2 us (level)
  no operation moved by 1% of the time
where the time goes in v7:
time: 18.2 us; the launch traced here: 18.1 us
  Pallas kernels  17.4 us (96%)
  between operations  0.64 us (4%)
    pallas_call x1, Pallas kernels, local(): pl.pallas_call(functools.partial(kernel, elems, params, inner), out_shape...  16.5 us
    pallas_call x1, Pallas kernels, local(): pl.pallas_call(finish_kernel, out_shape=(jax.ShapeDtypeStruct((modes, sna...  0.88 us

profile of v7, /device:TPU:0, one launch (start us, length us, event | category | flops | bytes accessed | tf_op | source)
XLA Modules:
  0.0 18.1 jit_solution(6369717473011889952)
XLA Ops:
  0.6 16.5 %shard_map.68 = (f32[2400,128]{1,0:T(8,128)S(1)}, f32[8,128]{1,0:T(8,128)S(1)}, f32[8,300]{1,0:T(8,128)S(1)}) custom-call(bf16[4,300]{1,0:T(4,128)(2,1)} %coords_hbm.1, bf16[3,300,256]{2,1,0:T(8,128)(2,1)} %basis_hbm.1, s32[8,128]{1,0:T(8,128)} %bitcast.3, f32[1,128]{1,0:T(1,128)} %bitcast.4, f32[24,24]{1,0:T(8,128)} %stiff_hbm.1), custom_call_target="tpu_custom_call" | custom-call | tf_op jit(solution)/shard_map/pallas_call | solution.py:572
  17.2 0.9 %shard_map.69 = (bf16[300,8,128]{2,1,0:T(8,128)(2,1)}, f32[8,300]{1,0:T(8,128)}) custom-call(f32[2400,128]{1,0:T(8,128)S(1)} %get-tuple-element.7.cols_ref, f32[8,128]{1,0:T(8,128)S(1)} %get-tuple-element.8.inverse_ref, f32[8,300]{1,0:T(8,128)S(1)} %get-tuple-element.9.target_ref), custom_call_target="tpu_custom_call" | custom-call | tf_op jit(solution)/shard_map/pallas_call | solution.py:615

commit v8 on v7

--- a/solution.py
+++ b/solution.py
@@ -12,7 +12,7 @@
 F32 = jnp.float32
 BF16 = jnp.bfloat16
 UNROLL = 64
-CHUNKS = 5
+CHUNKS = 4
 FAR = 2
 
 
@@ -37,10 +37,10 @@
     norms, part_p, part_e, total_ref, relay_disp, relay_ghost,
     load, load_b, send_g, recv_g, recv_d, recv_n, send_f, recv_f,
     recv_c, recv_p, recv_e, send_t, recv_t,
-    send_rd, recv_rd, send_rg, recv_rg, climb, known,
+    send_rd, recv_rd, recv_rg, climb, known,
 ):
     send_d, send_n, send_p, send_e = [load.at[i] for i in range(4)]
-    send_c = load_b
+    send_c, send_rg = load_b, send_p
     own_snaps, modes = coords_hbm.shape
     dofs = stiff_hbm.shape[0]
     snaps = own_snaps * params
@@ -602,7 +602,7 @@
             pltpu.VMEM(packed, BF16),
             dma((4,)), dma, dma, dma((CHUNKS,)), dma, dma, dma((params - 1,)), dma((2,)),
             dma, dma, dma, dma((params - 1,)), dma,
-            dma((params,)), dma, dma, dma((CHUNKS,)),
+            dma((params,)), dma, dma((CHUNKS,)),
             pltpu.SemaphoreType.REGULAR, pltpu.SemaphoreType.REGULAR,
         ],
         compiler_params=pltpu.CompilerParams(

time: 18.2 us -> 18.2 us (level)
  no operation moved by 1% of the time
where the time goes in v8:
time: 18.2 us; the launch traced here: 18.1 us
  Pallas kernels  17.4 us (96%)
  between operations  0.64 us (4%)
    pallas_call x1, Pallas kernels, local(): pl.pallas_call(functools.partial(kernel, elems, params, inner), out_shape...  16.5 us
    pallas_call x1, Pallas kernels, local(): pl.pallas_call(finish_kernel, out_shape=(jax.ShapeDtypeStruct((modes, sna...  0.88 us

profile of v8, /device:TPU:0, one launch (start us, length us, event | category | flops | bytes accessed | tf_op | source)
XLA Modules:
  0.0 18.1 jit_solution(13465836192941767519)
XLA Ops:
  0.6 16.5 %shard_map.68 = (f32[2400,128]{1,0:T(8,128)S(1)}, f32[8,128]{1,0:T(8,128)S(1)}, f32[8,300]{1,0:T(8,128)S(1)}) custom-call(bf16[4,300]{1,0:T(4,128)(2,1)} %coords_hbm.1, bf16[3,300,256]{2,1,0:T(8,128)(2,1)} %basis_hbm.1, s32[8,128]{1,0:T(8,128)} %bitcast.3, f32[1,128]{1,0:T(1,128)} %bitcast.4, f32[24,24]{1,0:T(8,128)} %stiff_hbm.1), custom_call_target="tpu_custom_call" | custom-call | tf_op jit(solution)/shard_map/pallas_call | solution.py:572
  17.2 0.9 %shard_map.69 = (bf16[300,8,128]{2,1,0:T(8,128)(2,1)}, f32[8,300]{1,0:T(8,128)}) custom-call(f32[2400,128]{1,0:T(8,128)S(1)} %get-tuple-element.7.cols_ref, f32[8,128]{1,0:T(8,128)S(1)} %get-tuple-element.8.inverse_ref, f32[8,300]{1,0:T(8,128)S(1)} %get-tuple-element.9.target_ref), custom_call_target="tpu_custom_call" | custom-call | tf_op jit(solution)/shard_map/pallas_call | solution.py:615
